TPU v7x, 8 devices: a whole 2x2x1 slice. The times are simulated.
8 devices in a mesh: dp: 1 (over z), tp: 8 (over y, x, core).
Axes of the slice: x: 2, y: 2, z: 1, core: 2. Of those that a mesh axis runs over, the one named last changes fastest.
Arguments:
- hidden: bfloat16 [128, 2048], P('dp')
- w_gate: bfloat16 [2048, 8192], P(None, 'tp')
- w_up: bfloat16 [2048, 8192], P(None, 'tp')
- w_down: bfloat16 [8192, 2048], P('tp')
- norm_gain: float32 [2048], replicated
- w_vocab: bfloat16 [2048, 49152], P(None, 'tp')
- temperature: float32 [128], P('dp')
- target: int32 [128], P('dp')
Outputs:
- output 1: float32 [128], P('dp')
- output 2: float32 [128], P('dp')
- output 3: float32 [128], P('dp')
- output 4: bfloat16 [128, 49152], P('dp')
All inputs are finite; a program needn't handle non-finite values.
Results may differ from a plain program's by a relative error of at most 0.00406014.
Values are sent between devices in bfloat16 or wider.
A program may use at most 1 GiB of HBM per device.

v0:
```python
import jax
import jax.numpy as jnp
from jax import lax
from jax.sharding import PartitionSpec as P

NORM_EPS = 1e-6


def solution(mesh):
    def device_step(hidden, w_gate, w_up, w_down, norm_gain, w_vocab, value_a11, target):
        gate_pre = jnp.dot(hidden, w_gate, preferred_element_type=jnp.float32)
        up_pre = jnp.dot(hidden, w_up, preferred_element_type=jnp.float32)
        hidden_act = (jax.nn.silu(gate_pre) * up_pre).astype(jnp.bfloat16)
        part_sum = jnp.dot(hidden_act, w_down, preferred_element_type=jnp.float32).astype(jnp.bfloat16)
        mlp_out = lax.psum(part_sum, "tp")
        residual = hidden.astype(jnp.float32) + mlp_out.astype(jnp.float32)
        inv_rms = lax.rsqrt(jnp.mean(residual * residual, axis=-1, keepdims=True) + NORM_EPS)
        normed = (norm_gain * residual * inv_rms).astype(jnp.bfloat16)
        logits = jnp.dot(normed, w_vocab, preferred_element_type=jnp.float32) / value_a11[:, None]
        vocab_local = logits.shape[1]
        row_max = lax.pmax(jnp.max(logits, axis=-1), "tp")
        shifted = jnp.exp(logits - row_max[:, None])
        local_ids = target - lax.axis_index("tp") * vocab_local
        col_ids = jnp.arange(vocab_local, dtype=jnp.int32)
        target_hit = jnp.where(col_ids[None, :] == local_ids[:, None], logits, 0.0)
        local_stats = jnp.stack(
            [jnp.sum(shifted, axis=-1), jnp.sum(shifted * logits, axis=-1), jnp.sum(target_hit, axis=-1)], axis=0)
        row_stats = lax.psum(local_stats, "tp")
        sum_exp = row_stats[0]
        weighted_sum = row_stats[1]
        target_logit = row_stats[2]
        log_norm = row_max + jnp.log(sum_exp)
        entropy = log_norm - weighted_sum / sum_exp
        target_logp = target_logit - log_norm
        local_probs = (logits - log_norm[:, None]).astype(jnp.bfloat16)
        log_probs = lax.all_gather(local_probs, "tp", axis=1, tiled=True)
        return log_norm, entropy, target_logp, log_probs

    return jax.shard_map(
        device_step,
        mesh=mesh,
        in_specs=(P("dp", None), P(None, "tp"), P(None, "tp"), P("tp", None), P(None),
                  P(None, "tp"), P("dp"), P("dp")),
        out_specs=(P("dp"), P("dp"), P("dp"), P("dp", None)),
        check_vma=False,
    )
```

profile of v0, /device:TPU:0, one launch (start us, length us, event | category | flops | bytes accessed | tf_op | source)
XLA Modules:
  0.0 208.1 jit_solution(5651070634847029207)
XLA Ops:
  7.2 0.0 copy-start
  7.2 0.0 all-reduce.2.cloned.1.call-start
  7.2 3.1 %fusion.12 = f32[128,1024]{1,0:T(8,128)S(1)} fusion(bf16[128,2048]{1,0:T(8,128)(2,1)} %param.8, bf16[2048,1024]{1,0:T(8,128)(2,1)} %param.9), kind=kOutput, calls=%fused_computation.30 | convolution fusion | flops 536870912 | bytes 5242880 | tf_op jit(solution)/shard_map/dot_general | solution.py:11
  10.3 0.0 copy-done
  10.3 0.0 copy-start.3
  10.4 0.0 copy-start.2
  10.4 0.0 copy-start.4
  10.4 5.6 %convolution_convert_fusion = bf16[128,2048]{1,0:T(8,128)(2,1)} fusion(bf16[1024,2048]{1,0:T(8,128)(2,1)} %param.11, bf16[128,2048]{1,0:T(8,128)(2,1)S(1)} %copy-done, bf16[2048,1024]{1,0:T(8,128)(2,1)} %param.10, f32[128,1024]{1,0:T(8,128)S(1)} %fusion.12), kind=kOutput, calls=%fused_computation.7 | convolution fusion | flops 1074790400 | bytes 9961472 | tf_op jit(solution)/shard_map/dot_general | solution.py:14
  16.0 0.0 all-reduce.2.cloned.1.call-update
  16.0 0.0 all-gather.2.cloned.1.call-start
  16.1 0.0 copy-done.3
  16.1 46.2 %all-reduce.2.cloned.1.call-done = bf16[128,2048]{1,0:T(8,128)(2,1)} async-done(((bf16[128,2048]{1,0:T(8,128)(2,1)}), bf16[128,2048]{1,0:T(8,128)(2,1)}) %all-reduce.2.cloned.1.call-update) | async-done | bytes 524304 | tf_op jit(solution)/shard_map/psum | solution.py:15
  62.3 1.3 multiply_reduce_fusion.1
  63.6 0.0 copy-done.2
  63.7 0.0 copy-done.4
  63.7 10.5 %fusion.11 = (f32[128]{0:T(128)S(1)}, f32[128,6144]{1,0:T(8,128)S(1)}) fusion(f32[128]{0:T(128)S(1)} %copy-done.4, bf16[2048,6144]{1,0:T(8,128)(2,1)} %param.13, bf16[128,2048]{1,0:T(8,128)(2,1)} %all-reduce.2.cloned.1.call-done, bf16[128,2048]{1,0:T(8,128)(2,1)} %param.8, f32[128]{0:T(128)S(1)} %add_rsqrt_fusion, f32[2048]{0:T(1024)S(1)} %copy-done.2), kind=kOutput, calls=%fused_computation.29 | convolution fusion | flops 3224371200 | bytes 29369856 | tf_op jit(solution)/shard_map/dot_general | solution.py:19
  74.2 22.2 %pmax.7 = f32[128]{0:T(128)S(1)} all-reduce(f32[128]{0:T(128)S(1)} %get-tuple-element.9), channel_id=1, replica_groups=mesh['dp'=1,'tp'=8] {'tp'}, use_global_device_ids=true, to_apply=%region_3.4 | all-reduce | flops 128 | bytes 1024 | tf_op jit(solution)/shard_map/pmax | solution.py:21
  96.4 1.2 fusion
  97.6 23.3 %psum.15 = f32[3,128]{1,0:T(4,128)S(1)} all-reduce(f32[3,128]{1,0:T(4,128)S(1)} %pad_maximum_fusion), channel_id=1, replica_groups=mesh['dp'=1,'tp'=8] {'tp'}, use_global_device_ids=true, to_apply=%region_7.8 | all-reduce | flops 384 | bytes 3072 | tf_op jit(solution)/shard_map/psum | solution.py:28
  120.9 0.5 bitcast_subtract_fusion
  121.4 0.0 copy-start.1
  121.4 1.4 subtract_convert_fusion
  122.8 0.0 all-gather.2.cloned.1.call-update
  122.9 0.5 bitcast_subtract_fusion.1
  123.4 67.4 %all-gather.2.cloned.1.call-done = bf16[128,49152]{1,0:T(8,128)(2,1)} async-done(((bf16[128,6144]{1,0:T(8,128)(2,1)}), bf16[128,49152]{1,0:T(8,128)(2,1)}) %all-gather.2.cloned.1.call-update) | async-done | bytes 12582928 | tf_op jit(solution)/shard_map/all_gather | solution.py:36
  190.8 10.4 %copy.14 = bf16[128,49152]{1,0:T(8,128)(2,1)} copy(bf16[128,49152]{1,0:T(8,128)(2,1)} %all-gather.2.cloned.1.call-done) | data formatting | bytes 25165824
  201.2 0.0 copy-done.1
  (3 shorter events, 0.0 us)
Async XLA Ops:
  7.2 3.2 %copy-start = (bf16[128,2048]{1,0:T(8,128)(2,1)S(1)}, bf16[128,2048]{1,0:T(8,128)(2,1)}, u32[]{:S(2)}) copy-start(bf16[128,2048]{1,0:T(8,128)(2,1)} %param.8) | copy-start | bytes 1572868
  7.2 55.2 %all-reduce.2.cloned.1.call-start = ((), (), s32[]{:S(2)}) async-start(), calls=%async_computation | async-start | bytes 1048576 | tf_op jit(solution)/shard_map/psum | solution.py:15
  10.3 5.7 %copy-start.3 = (s32[128]{0:T(128)S(1)}, s32[128]{0:T(128)}, u32[]{:S(2)}) copy-start(s32[128]{0:T(128)} %param.15) | copy-start | bytes 1540
  10.4 53.3 %copy-start.2 = (f32[2048]{0:T(1024)S(1)}, f32[2048]{0:T(1024)}, u32[]{:S(2)}) copy-start(f32[2048]{0:T(1024)} %param.12) | copy-start | bytes 24580
  10.4 53.3 %copy-start.4 = (f32[128]{0:T(128)S(1)}, f32[128]{0:T(128)}, u32[]{:S(2)}) copy-start(f32[128]{0:T(128)} %param.14) | copy-start | bytes 1540
  16.0 174.8 %all-gather.2.cloned.1.call-start = ((), (), s32[]{:S(2)}) async-start(), calls=%async_computation.1 | async-start | bytes 14155776 | tf_op jit(solution)/shard_map/all_gather | solution.py:36
  121.4 79.8 %copy-start.1 = (f32[128]{0:T(128)}, f32[128]{0:T(128)S(1)}, u32[]{:S(2)}) copy-start(f32[128]{0:T(128)S(1)} %get-tuple-element.15) | copy-start | bytes 1540
Sparse Core Ops, SparseCore 0:
  16.2 46.1 all-reduce.1
  123.0 67.7 all-gather.1
where the time goes:
time: 209 us; the launch traced here: 208 us
  waiting for transfers between devices  114 us (55%)
  blocking collectives  45.5 us (22%)
  matrix products  19.2 us (9%)
  between operations  14.1 us (7%)
  local copies, waits for them, and re-layouts  10.5 us (5%)
  other arithmetic  4.94 us (2%)
    all_gather x1, waiting for transfers between devices, device_step(): log_probs = lax.all_gather(local_probs, 'tp', axis=1, tiled=True)  67.4 us
    psum x1, waiting for transfers between devices, device_step(): mlp_out = lax.psum(part_sum, 'tp')  46.2 us
    psum x1, blocking collectives, device_step(): row_stats = lax.psum(local_stats, 'tp')  23.3 us
    pmax x1, blocking collectives, device_step(): row_max = lax.pmax(jnp.max(logits, axis=-1), 'tp')  22.2 us
    dot_general x1, matrix products, device_step(): jnp.dot(normed, w_vocab, preferred_element_type=jnp.float32)  10.5 us
    unnamed x11, local copies, waits for them, and re-layouts  10.5 us
    dot_general x1, matrix products, device_step(): jnp.dot(hidden_act, w_down, preferred_element_type=jnp.float32)  5.62 us
  transfers between devices with their start and end apart: 2, of which 2 were waited for; matrix products, arithmetic and copies ran while one was open for 0% of the time, Pallas kernels for 0%

commit v1 on v0

v1 whole, which is shorter than its diff:
```python
import jax
import jax.numpy as jnp
from jax import lax
from jax.experimental import pallas as pl
from jax.experimental.pallas import tpu as pltpu
from jax.sharding import PartitionSpec as P

NORM_EPS = 1e-6
F32 = jnp.float32
BF16 = jnp.bfloat16
B, D, FL, V, VL = 128, 2048, 1024, 49152, 6144
NC = 12
CW = VL // NC
EARLY = 3
NF = 4
FW = FL // NF
NJ = 2
JW = D // NJ
HALF, PIECE = 64, 16


def _lanes(row):
    return jnp.transpose(jnp.broadcast_to(row, (128, 128)))


def _main(hid_hbm, wg_hbm, wu_hbm, wd_hbm, gain_ref, wv_hbm, temp_ref, tgt_ref,
          out, small,
          w, wv, hid, act, yf, ysend, yrecv, psend, precv, xbuf, statm, stats, offs, invt, tgtm,
          in_sem, wf_sem, wd_sem, wv_sem,
          d2d_s, d2d_r, rs_s, rs_r, xa_s, xa_r, xf_s, xf_r, st_s, st_r,
          own_s, fwd_s, par_s, rx, ry, rd, pr):
    me = lax.axis_index("tp")
    core, chip = me % 2, me // 2
    nx, ny, nd, pt = me ^ 2, me ^ 4, me ^ 6, me ^ 1

    def remote(src, dst, ss, rs, dev):
        return pltpu.make_async_remote_copy(src, dst, ss, rs, device_id={"tp": dev})

    hid_copy = pltpu.make_async_copy(hid_hbm, hid, in_sem)
    hid_copy.start()
    wf_copies = []
    for b in range(NF):
        for t, ref in enumerate((wg_hbm, wu_hbm)):
            c = pltpu.make_async_copy(ref.at[:, pl.ds(b * FW, FW)], w.at[:, pl.ds(t * FL + b * FW, FW)], wf_sem.at[t, b])
            c.start()
            wf_copies.append(c)
    wd_copies = []
    for j in range(NJ):
        c = pltpu.make_async_copy(wd_hbm.at[:, pl.ds(j * JW, JW)], w.at[pl.ds(j * FL, FL), pl.ds(2 * FL, JW)], wd_sem.at[j])
        c.start()
        wd_copies.append(c)

    barrier = pltpu.get_barrier_semaphore()
    for k in range(1, 8):
        pl.semaphore_signal(barrier, inc=1, device_id={"tp": me ^ k})

    invt[...] = _lanes(1.0 / temp_ref[...])
    tgtm[...] = _lanes(tgt_ref[...].astype(F32)).astype(jnp.int32)

    hid_copy.wait()
    for b in range(NF):
        wf_copies[2 * b].wait()
        wf_copies[2 * b + 1].wait()
        g = jnp.dot(hid[...], w[:, b * FW:(b + 1) * FW], preferred_element_type=F32)
        u = jnp.dot(hid[...], w[:, FL + b * FW:FL + (b + 1) * FW], preferred_element_type=F32)
        act[:, b * FW:(b + 1) * FW] = (jax.nn.silu(g) * u).astype(BF16)

    keep = pl.multiple_of(core * HALF, HALF)
    give = pl.multiple_of(HALF - core * HALF, HALF)
    d2d = []
    for j in range(NJ):
        cols = pl.ds(j * JW, JW)
        wd_copies[j].wait()
        yf[:, j * JW:(j + 1) * JW] = jnp.dot(act[...], w[j * FL:(j + 1) * FL, 2 * FL:2 * FL + JW], preferred_element_type=F32)
        ysend[:, j * JW:(j + 1) * JW] = yf[pl.ds(give, HALF), j * JW:(j + 1) * JW].astype(BF16)
        if j == 0:
            pl.semaphore_wait(barrier, 7)
        c = remote(ysend.at[:, cols], yrecv.at[:, cols], d2d_s.at[j], d2d_r.at[j], pt)
        c.start()
        d2d.append(c)

    wv_copies = []
    for i in range(NC):
        c = pltpu.make_async_copy(wv_hbm.at[:, pl.ds(i * CW, CW)], wv.at[:, pl.ds(i * CW, CW)], wv_sem.at[i])
        c.start()
        wv_copies.append(c)

    def piece(dev):
        return pl.multiple_of((dev // 2) * PIECE, PIECE)

    rs = []
    for j in range(NJ):
        cols = slice(j * JW, (j + 1) * JW)
        d2d[j].wait_recv()
        part = yf[pl.ds(keep, HALF), cols] + yrecv[:, cols].astype(F32)
        yf[pl.ds(keep, HALF), cols] = part
        psend[:, cols] = part.astype(BF16)
        for s, dev in enumerate((nd, nx, ny)):
            c = remote(psend.at[pl.ds(piece(dev), PIECE), pl.ds(j * JW, JW)], precv.at[s, :, pl.ds(j * JW, JW)],
                       rs_s.at[s, j], rs_r.at[s, j], dev)
            c.start()
            rs.append(c)

    def rows_of(dev):
        return pl.multiple_of((dev % 2) * HALF + (dev // 2) * PIECE, PIECE)

    mine = rows_of(me)
    for c in rs:
        c.wait_recv()
    y = yf[pl.ds(mine, PIECE), :]
    for s in range(3):
        y = y + precv[s].astype(F32)
    res = hid[pl.ds(mine, PIECE), :].astype(F32) + y
    inv_rms = lax.rsqrt(jnp.mean(res * res, axis=-1, keepdims=True) + NORM_EPS)
    xbuf[pl.ds(mine, PIECE), :] = (gain_ref[...] * res * inv_rms).astype(BF16)

    def xrow(dev):
        return xbuf.at[pl.ds(rows_of(dev), PIECE), :]

    xs = []
    for s, dev in enumerate((nd, nx, ny)):
        xs.append(remote(xrow(me), xrow(me), xa_s.at[s], xa_r.at[s], dev))
    xs.append(remote(xrow(me), xrow(me), xf_s.at[3], xf_r.at[3], pt))
    for c in xs:
        c.start()
    xf = []
    for s, dev in ((1, nx), (2, ny), (0, nd)):
        remote(xrow(dev), xrow(dev), xa_s.at[s], xa_r.at[s], dev).wait_recv()
        c = remote(xrow(dev), xrow(dev), xf_s.at[s], xf_r.at[s], pt)
        c.start()
        xf.append(c)
    for s, dev in ((3, pt), (1, pt ^ 2), (2, pt ^ 4), (0, pt ^ 6)):
        remote(xrow(dev), xrow(dev), xf_s.at[s], xf_r.at[s], pt).wait_recv()

    def chunk(dev, i):
        row = pl.multiple_of((dev * 2 + i // 6) * 128, 128)
        col = pl.multiple_of((i % 6) * CW, CW)
        return w.at[pl.ds(row, 128), pl.ds(col, CW)]

    def own_copies(i):
        return (remote(chunk(me, i), chunk(me, i), own_s.at[0, i], rx.at[i], nx),
                remote(chunk(me, i), chunk(me, i), own_s.at[1, i], ry.at[i], ny),
                remote(chunk(me, i), chunk(me, i), own_s.at[2, i], pr.at[0, i], pt))

    lane = lax.broadcasted_iota(jnp.int32, (128, 128), 1)
    statm[...] = jnp.zeros((128, 128), F32)

    def head(i, _):
        pltpu.make_async_copy(wv_hbm.at[:, pl.ds(pl.multiple_of(i * CW, CW), CW)],
                              wv.at[:, pl.ds(pl.multiple_of(i * CW, CW), CW)], wv_sem.at[i]).wait()
        acc = jnp.dot(xbuf[...], wv[:, pl.ds(pl.multiple_of(i * CW, CW), CW)], preferred_element_type=F32)
        parts = [acc[:, q * 128:(q + 1) * 128] * invt[...] for q in range(CW // 128)]
        top = parts[0]
        for p in parts[1:]:
            top = jnp.maximum(top, p)
        top = jnp.max(top, axis=-1, keepdims=True)
        ref = chunk(me, i)
        for q, p in enumerate(parts):
            ref[:, q * 128:(q + 1) * 128] = (p - top).astype(BF16)

        @pl.when(i < EARLY)
        def _():
            for c in own_copies(i):
                c.start()

        total = weighted = hit = jnp.zeros((128, 128), F32)
        ids = tgtm[...] - (me * VL + i * CW)
        for q, p in enumerate(parts):
            e = jnp.exp(p - top)
            total = total + e
            weighted = weighted + e * p
            hit = hit + jnp.where(ids == lane + q * 128, p, 0.0)
        sm = statm[...]
        sm = jnp.where(lane == i, top, sm)
        sm = jnp.where(lane == 16 + i, jnp.sum(total, axis=-1, keepdims=True), sm)
        sm = jnp.where(lane == 32 + i, jnp.sum(weighted, axis=-1, keepdims=True), sm)
        sm = jnp.where(lane == 48 + i, jnp.sum(hit, axis=-1, keepdims=True), sm)
        statm[...] = sm
        return 0

    lax.fori_loop(0, NC, head, 0)

    st = jnp.transpose(statm[...])
    tops = st[0:NC, :]
    top = jnp.max(tops, axis=0, keepdims=True)
    scale = jnp.exp(tops - top)
    my_stats = jnp.concatenate(
        [tops, top, jnp.sum(scale * st[16:16 + NC, :], axis=0, keepdims=True),
         jnp.sum(scale * st[32:32 + NC, :], axis=0, keepdims=True),
         jnp.sum(st[48:48 + NC, :], axis=0, keepdims=True)], axis=0)

    def slot(dev):
        return stats.at[pl.ds(pl.multiple_of(dev * 16, 16), 16), :]

    slot(me)[...] = my_stats
    sts = []
    for k in range(1, 8):
        c = remote(slot(me), slot(me), st_s.at[k], st_r.at[k], me ^ k)
        c.start()
        sts.append(c)

    def send_rest(i, _):
        for c in own_copies(i):
            c.start()
        return 0

    lax.fori_loop(EARLY, NC, send_rest, 0)

    for k in range(1, 8):
        remote(slot(me ^ k), slot(me ^ k), st_s.at[k], st_r.at[k], me ^ k).wait_recv()
    allst = [stats[16 * k:16 * (k + 1), :] for k in range(8)]
    top = allst[0][12:13, :]
    for s in allst[1:]:
        top = jnp.maximum(top, s[12:13, :])
    total = weighted = hit = jnp.zeros((1, 128), F32)
    for s in allst:
        scale = jnp.exp(s[12:13, :] - top)
        total = total + scale * s[13:14, :]
        weighted = weighted + scale * s[14:15, :]
        hit = hit + s[15:16, :]
    log_norm = top + jnp.log(total)
    small[0:1, :] = log_norm
    small[1:2, :] = log_norm - weighted / total
    small[2:3, :] = hit - log_norm
    small[3:8, :] = jnp.zeros((5, 128), F32)
    offs[...] = jnp.transpose(stats[...] - log_norm)

    def fix(dev, i):
        off = jnp.sum(jnp.where(lane == dev * 16 + i, offs[...], 0.0), axis=-1, keepdims=True)
        val = chunk(dev, i)[...].astype(F32) + off
        out[:, pl.ds(pl.multiple_of(dev * VL + i * CW, CW), CW)] = val.astype(BF16)

    def from_partner(j, dev, i):
        remote(chunk(dev, i), chunk(dev, i), par_s.at[0, i], pr.at[j, i], pt).wait_recv()
        fix(dev, i)

    def to_partner(j, dev, i):
        remote(chunk(dev, i), chunk(dev, i), par_s.at[j, i], pr.at[j + 1, i], pt).start()

    def relay(dev, i, to):
        return remote(chunk(dev, i), chunk(dev, i), fwd_s.at[i], rd.at[i], to)

    def arrivals(i, _):
        remote(chunk(nx, i), chunk(nx, i), own_s.at[0, i], rx.at[i], nx).wait_recv()

        @pl.when(i % 2 == 0)
        def _():
            relay(nx, i, ny).start()

        to_partner(0, nx, i)
        remote(chunk(ny, i), chunk(ny, i), own_s.at[1, i], ry.at[i], ny).wait_recv()

        @pl.when(i % 2 == 1)
        def _():
            relay(ny, i, nx).start()

        to_partner(1, ny, i)
        fix(me, i)
        fix(nx, i)
        fix(ny, i)
        from_partner(0, pt, i)
        from_partner(1, pt ^ 2, i)
        from_partner(2, pt ^ 4, i)
        return 0

    lax.fori_loop(0, NC, arrivals, 0)

    def diagonal(i, _):
        remote(chunk(nd, i), chunk(nd, i), fwd_s.at[i], rd.at[i], nx).wait_recv()
        to_partner(2, nd, i)
        fix(nd, i)
        from_partner(3, pt ^ 6, i)
        return 0

    lax.fori_loop(0, NC, diagonal, 0)

    def drain(i, _):
        for c in own_copies(i):
            c.wait_send()
        relay(nx, i, ny).wait_send()
        for j, dev in enumerate((nx, ny, nd)):
            remote(chunk(dev, i), chunk(dev, i), par_s.at[j, i], pr.at[j + 1, i], pt).wait_send()
        return 0

    lax.fori_loop(0, NC, drain, 0)
    for c in d2d + rs + xs + xf + sts:
        c.wait_send()


def _write(src, small, out, o0, o1, o2, sem):
    step = B // 8
    cs = [pltpu.make_async_copy(src.at[pl.ds(k * step, step)], out.at[pl.ds(k * step, step)], sem.at[k]) for k in range(8)]
    for c in cs:
        c.start()
    o0[...] = small[0:1, :]
    o1[...] = small[1:2, :]
    o2[...] = small[2:3, :]
    for c in cs:
        c.wait()


def solution(mesh):
    vmem = pl.BlockSpec(memory_space=pltpu.VMEM)
    hbm = pl.BlockSpec(memory_space=pltpu.HBM)
    dma = pltpu.SemaphoreType.DMA

    def device_step(hidden, w_gate, w_up, w_down, norm_gain, w_vocab, temperature, target):
        wide, small = pl.pallas_call(
            _main,
            out_shape=(pltpu.VMEM((B, V), BF16), pltpu.VMEM((8, 128), F32)),
            in_specs=[hbm, hbm, hbm, hbm, vmem, hbm, vmem, vmem],
            out_specs=(vmem, vmem),
            scratch_shapes=[
                pltpu.VMEM((2048, 3072), BF16), pltpu.VMEM((D, VL), BF16), pltpu.VMEM((B, D), BF16),
                pltpu.VMEM((B, FL), BF16), pltpu.VMEM((B, D), F32), pltpu.VMEM((HALF, D), BF16),
                pltpu.VMEM((HALF, D), BF16), pltpu.VMEM((HALF, D), BF16), pltpu.VMEM((3, PIECE, D), BF16),
                pltpu.VMEM((B, D), BF16), pltpu.VMEM((128, 128), F32), pltpu.VMEM((128, 128), F32),
                pltpu.VMEM((128, 128), F32), pltpu.VMEM((128, 128), F32), pltpu.VMEM((128, 128), jnp.int32),
                dma, dma((2, NF)), dma((NJ,)), dma((NC,)),
                dma((NJ,)), dma((NJ,)), dma((3, NJ)), dma((3, NJ)), dma((3,)), dma((3,)), dma((4,)), dma((4,)),
                dma((8,)), dma((8,)),
                dma((3, NC)), dma((NC,)), dma((3, NC)), dma((NC,)), dma((NC,)), dma((NC,)), dma((4, NC)),
            ],
            compiler_params=pltpu.CompilerParams(collective_id=0, has_side_effects=True, vmem_limit_bytes=49 << 20),
            name="step",
        )(hidden, w_gate, w_up, w_down, norm_gain.reshape(1, D), w_vocab, temperature.reshape(1, B), target.reshape(1, B))
        row = jax.ShapeDtypeStruct((1, B), F32)
        log_probs, log_norm, entropy, target_logp = pl.pallas_call(
            _write,
            out_shape=(jax.ShapeDtypeStruct((B, V), BF16), row, row, row),
            in_specs=[vmem, vmem],
            out_specs=(hbm, vmem, vmem, vmem),
            scratch_shapes=[dma((8,))],
            compiler_params=pltpu.CompilerParams(vmem_limit_bytes=16 << 20),
            name="write",
        )(wide, small)
        return log_norm.reshape(B), entropy.reshape(B), target_logp.reshape(B), log_probs

    return jax.shard_map(
        device_step,
        mesh=mesh,
        in_specs=(P("dp", None), P(None, "tp"), P(None, "tp"), P("tp", None), P(None),
                  P(None, "tp"), P("dp"), P("dp")),
        out_specs=(P("dp"), P("dp"), P("dp"), P("dp", None)),
        check_vma=False,
    )
```

time: 209 us -> 85.5 us (0.41)
  waiting for transfers between devices: 114 us -> 0 us
  Pallas kernels: 0 us -> 84.8 us
  blocking collectives: 45.5 us -> 0 us
  matrix products: 19.2 us -> 0 us
  between operations: 14.1 us -> 0.64 us
  local copies, waits for them, and re-layouts: 10.5 us -> 0 us
  other arithmetic: 4.94 us -> 0 us
    pallas_call x0 -> x2, Pallas kernels: none -> 84.8 us  [the longest x1 79.6 us: device_step(): pl.pallas_call(_main, out_shape=(pltpu.VMEM((B, V), BF16), pltpu.VMEM((8,...]
    all_gather x1 -> x0, waiting for transfers between devices: 67.4 us -> none  [device_step(): log_probs = lax.all_gather(local_probs, 'tp', axis=1, tiled=True)]
    psum x1 -> x0, waiting for transfers between devices: 46.2 us -> none  [device_step(): mlp_out = lax.psum(part_sum, 'tp')]
    psum x1 -> x0, blocking collectives: 23.3 us -> none  [device_step(): row_stats = lax.psum(local_stats, 'tp')]
    pmax x1 -> x0, blocking collectives: 22.2 us -> none  [device_step(): row_max = lax.pmax(jnp.max(logits, axis=-1), 'tp')]
    dot_general x3 -> x0, matrix products: 19.2 us -> none  [the longest x1 10.5 us: device_step(): jnp.dot(normed, w_vocab, preferred_element_type=jnp.float32)]
    unnamed x11 -> x0, local copies, waits for them, and re-layouts: 10.5 us -> none
    reduce_sum x2 -> x0, other arithmetic: 2.45 us -> none  [the longest x1 1.29 us: device_step(): jnp.mean(residual * residual, axis=-1, keepdims=True) + NORM_EPS]
  transfers between devices with their start and end apart: 2 -> 0, of which waited for: 2 -> 0; matrix products, arithmetic and copies ran while one was open for 0% -> 0% of each run, Pallas kernels for 0% -> 0%
where the time goes in v1:
time: 85.5 us; the launch traced here: 85.4 us
  Pallas kernels  84.8 us (99%)
    pallas_call x1, Pallas kernels, device_step(): pl.pallas_call(_main, out_shape=(pltpu.VMEM((B, V), BF16), pltpu.VMEM((8,...  79.6 us
    pallas_call x1, Pallas kernels, device_step(): pl.pallas_call(_write, out_shape=(jax.ShapeDtypeStruct((B, V), BF16), row...  5.18 us

profile of v1, /device:TPU:0, one launch (start us, length us, event | category | flops | bytes accessed | tf_op | source)
XLA Modules:
  0.0 85.4 jit_solution(5663069715271671725)
XLA Ops:
  0.6 79.6 %step.1 = (bf16[128,49152]{1,0:T(8,128)(2,1)S(1)}, f32[8,128]{1,0:T(8,128)S(1)}) custom-call(bf16[128,2048]{1,0:T(8,128)(2,1)} %hid_hbm.1, bf16[2048,1024]{1,0:T(8,128)(2,1)} %wg_hbm.1, bf16[2048,1024]{1,0:T(8,128)(2,1)} %wu_hbm.1, bf16[1024,2048]{1,0:T(8,128)(2,1)} %wd_hbm.1, f32[1,2048]{1,0:T(1,128)} %bitcast.6, bf16[2048,6144]{1,0:T(8,128)(2,1)} %wv_hbm.1, ...), custom_call_target="tpu_custom_call" | custom-call | tf_op jit(solution)/shard_map/step/pallas_call | solution.py:308
  80.2 5.2 %write.1 = (bf16[128,49152]{1,0:T(8,128)(2,1)}, f32[1,128]{1,0:T(1,128)}, f32[1,128]{1,0:T(1,128)}, f32[1,128]{1,0:T(1,128)}) custom-call(bf16[128,49152]{1,0:T(8,128)(2,1)S(1)} %get-tuple-element.10.src, f32[8,128]{1,0:T(8,128)S(1)} %get-tuple-element.11.small), custom_call_target="tpu_custom_call" | custom-call | tf_op jit(solution)/shard_map/write/pallas_call | solution.py:328

commit v2 on v1

v2 whole, which is shorter than its diff:
```python
import jax
import jax.numpy as jnp
from jax import lax
from jax.experimental import pallas as pl
from jax.experimental.pallas import tpu as pltpu
from jax.sharding import PartitionSpec as P

NORM_EPS = 1e-6
F32 = jnp.float32
BF16 = jnp.bfloat16
B, D, FL, V, VL = 128, 2048, 1024, 49152, 6144
NC = 8
CW = VL // NC
GRID = 3072 // CW
EARLY = 3
NF = 4
FW = FL // NF
NJ = 2
JW = D // NJ
HALF, PIECE = 64, 16
NW = 4
WW = VL // NW


def _lanes(row):
    return jnp.transpose(jnp.broadcast_to(row, (128, 128)))


def _main(hid_hbm, wg_hbm, wu_hbm, wd_hbm, gain_hbm, wv_hbm, temp_hbm, tgt_hbm,
          out, small,
          w, wv, hid, act, yf, ysend, yrecv, psend, precv, xbuf, statm, stats, offs, invt, tgtm, gain, temp, tgt,
          in_sem, wf_sem, wd_sem, wv_sem,
          d2d_s, d2d_r, rs_s, rs_r, x_s, xa_r, xf_r, st_s, st_r, bulk_s, rxy, rd, pr, prd):
    me = lax.axis_index("tp")
    core = me % 2
    nx, ny, nd, pt = me ^ 2, me ^ 4, me ^ 6, me ^ 1

    def remote(src, dst, ss, rs, dev):
        return pltpu.make_async_remote_copy(src, dst, ss, rs, device_id={"tp": dev})

    def load(src, dst, sem):
        c = pltpu.make_async_copy(src, dst, sem)
        c.start()
        return c

    def load_wf(b):
        for t, ref in enumerate((wg_hbm, wu_hbm)):
            load(ref.at[:, pl.ds(b * FW, FW)], w.at[:, pl.ds(t * FL + b * FW, FW)], wf_sem.at[b])

    def wait_wf(b):
        both = w.at[:, pl.ds(0, 2 * FW)]
        pltpu.make_async_copy(wv_hbm.at[:, pl.ds(0, 2 * FW)], both, wf_sem.at[b]).wait()

    def load_wd(j):
        return load(wd_hbm.at[:, pl.ds(j * JW, JW)], w.at[pl.ds(j * FL, FL), pl.ds(2 * FL, JW)], wd_sem.at[j])

    def load_wv(n):
        return load(wv_hbm.at[:, pl.ds(n * WW, WW)], wv.at[:, pl.ds(n * WW, WW)], wv_sem.at[n])

    hid_copy = load(hid_hbm, hid, in_sem.at[0])
    load_wf(0)
    small_copies = [load(temp_hbm, temp, in_sem.at[1]), load(tgt_hbm, tgt, in_sem.at[2]), load(gain_hbm, gain, in_sem.at[3])]
    load_wf(1)

    barrier = pltpu.get_barrier_semaphore()
    for k in range(1, 8):
        pl.semaphore_signal(barrier, inc=1, device_id={"tp": me ^ k})

    hid_copy.wait()
    wd_copies, wv_copies = [], []
    for b in range(NF):
        wait_wf(b)
        if b < NF - 2:
            load_wf(b + 2)
        else:
            wd_copies.append(load_wd(b - NF + 2))
        g = jnp.dot(hid[...], w[:, b * FW:(b + 1) * FW], preferred_element_type=F32)
        u = jnp.dot(hid[...], w[:, FL + b * FW:FL + (b + 1) * FW], preferred_element_type=F32)
        act[:, b * FW:(b + 1) * FW] = (jax.nn.silu(g) * u).astype(BF16)

    keep = pl.multiple_of(core * HALF, HALF)
    give = pl.multiple_of(HALF - core * HALF, HALF)
    d2d = []
    for j in range(NJ):
        cols = pl.ds(j * JW, JW)
        wd_copies[j].wait()
        wv_copies.append(load_wv(j))
        yf[:, j * JW:(j + 1) * JW] = jnp.dot(act[...], w[j * FL:(j + 1) * FL, 2 * FL:2 * FL + JW], preferred_element_type=F32)
        ysend[:, j * JW:(j + 1) * JW] = yf[pl.ds(give, HALF), j * JW:(j + 1) * JW].astype(BF16)
        if j == 0:
            pl.semaphore_wait(barrier, 7)
        c = remote(ysend.at[:, cols], yrecv.at[:, cols], d2d_s, d2d_r.at[j], pt)
        c.start()
        d2d.append(c)

    def rows_of(dev):
        return pl.multiple_of((dev % 2) * HALF + (dev // 2) * PIECE, PIECE)

    for c in small_copies:
        c.wait()
    offs[...] = _lanes(1.0 / temp[...])
    statm[...] = _lanes(tgt[...].astype(F32))
    for k in range(8):
        rows = pl.ds(rows_of(me ^ k), PIECE)
        invt[k * PIECE:(k + 1) * PIECE, :] = offs[rows, :]
        tgtm[k * PIECE:(k + 1) * PIECE, :] = statm[rows, :].astype(jnp.int32)

    def piece(dev):
        return pl.multiple_of((dev // 2) * PIECE, PIECE)

    for j in range(NJ):
        cols = slice(j * JW, (j + 1) * JW)
        d2d[j].wait_recv()
        part = yf[pl.ds(keep, HALF), cols] + yrecv[:, cols].astype(F32)
        yf[pl.ds(keep, HALF), cols] = part
        psend[:, cols] = part.astype(BF16)
        for s, dev in enumerate((nd, nx, ny)):
            remote(psend.at[pl.ds(piece(dev), PIECE), pl.ds(j * JW, JW)], precv.at[pl.ds(s * PIECE, PIECE), pl.ds(j * JW, JW)],
                   rs_s, rs_r, dev).start()
    for n in range(NJ, NW):
        wv_copies.append(load_wv(n))

    rs_all = remote(precv, precv, rs_s, rs_r, nx)
    rs_all.wait_recv()
    mine = rows_of(me)
    y = yf[pl.ds(mine, PIECE), :]
    for s in range(3):
        y = y + precv[s * PIECE:(s + 1) * PIECE, :].astype(F32)
    res = hid[pl.ds(mine, PIECE), :].astype(F32) + y
    inv_rms = lax.rsqrt(jnp.mean(res * res, axis=-1, keepdims=True) + NORM_EPS)
    xbuf[0:PIECE, :] = (gain[...] * res * inv_rms).astype(BF16)

    def xrow(k):
        return xbuf.at[pl.ds(k * PIECE, PIECE), :]

    for s, k in enumerate((6, 2, 4)):
        remote(xrow(0), xrow(k), x_s, xa_r.at[s], me ^ k).start()
    remote(xrow(0), xrow(1), x_s, xf_r, pt).start()

    def place(dev, i):
        row = pl.multiple_of((dev * 2 + i // GRID) * 128, 128)
        col = pl.multiple_of((i % GRID) * CW, CW)
        return row, pl.ds(col, CW)

    def chunk(dev, i):
        row, cols = place(dev, i)
        return w.at[pl.ds(row, 128), cols]

    def own_start(i, first, count):
        row, cols = place(me, i)
        ref = w.at[pl.ds(row + first, count), cols]
        remote(ref, ref, bulk_s, rxy.at[i], nx).start()
        remote(ref, ref, bulk_s, rxy.at[i], ny).start()
        remote(ref, ref, bulk_s, pr.at[i], pt).start()

    def head(i, first, count):
        acc = jnp.dot(xbuf[first:first + count, :], wv[:, pl.ds(pl.multiple_of(i * CW, CW), CW)], preferred_element_type=F32)
        scale = invt[first:first + count, :]
        parts = [acc[:, q * 128:(q + 1) * 128] * scale for q in range(CW // 128)]
        top = parts[0]
        for p in parts[1:]:
            top = jnp.maximum(top, p)
        top = jnp.max(top, axis=-1, keepdims=True)
        row, _ = place(me, i)
        for q, p in enumerate(parts):
            w[pl.ds(row + first, count), pl.ds(pl.multiple_of((i % GRID) * CW + q * 128, 128), 128)] = (p - top).astype(BF16)
        if first == 0:
            own_start(i, first, count)
        else:
            @pl.when(i < EARLY)
            def _():
                own_start(i, first, count)

        total = weighted = hit = jnp.zeros((count, 128), F32)
        lane = lax.broadcasted_iota(jnp.int32, (count, 128), 1)
        ids = tgtm[first:first + count, :] - (me * VL + i * CW)
        for q, p in enumerate(parts):
            e = jnp.exp(p - top)
            total = total + e
            weighted = weighted + e * p
            hit = hit + jnp.where(ids == lane + q * 128, p, 0.0)
        sm = statm[first:first + count, :]
        sm = jnp.where(lane == i, top, sm)
        sm = jnp.where(lane == 16 + i, jnp.sum(total, axis=-1, keepdims=True), sm)
        sm = jnp.where(lane == 32 + i, jnp.sum(weighted, axis=-1, keepdims=True), sm)
        sm = jnp.where(lane == 48 + i, jnp.sum(hit, axis=-1, keepdims=True), sm)
        statm[first:first + count, :] = sm

    def head_own(i, _):
        head(i, 0, PIECE)
        return 0

    def head_rest(i, _):
        head(i, PIECE, B - PIECE)
        return 0

    for c in wv_copies:
        c.wait()
    lax.fori_loop(0, NC, head_own, 0)
    for s, k in ((1, 2), (2, 4), (0, 6)):
        remote(xrow(k), xrow(k), x_s, xa_r.at[s], me ^ k).wait_recv()
        remote(xrow(k), xrow(k + 1), x_s, xf_r, pt).start()
    four = xbuf.at[pl.ds(0, 4 * PIECE), :]
    remote(four, four, x_s, xf_r, pt).wait_recv()
    lax.fori_loop(0, NC, head_rest, 0)

    for k in range(8):
        offs[pl.ds(rows_of(me ^ k), PIECE), :] = statm[k * PIECE:(k + 1) * PIECE, :]
    st = jnp.transpose(offs[...])
    tops = st[0:NC, :]
    top = jnp.max(tops, axis=0, keepdims=True)
    scale = jnp.exp(tops - top)
    my_stats = jnp.concatenate(
        [tops, top, jnp.sum(scale * st[16:16 + NC, :], axis=0, keepdims=True),
         jnp.sum(scale * st[32:32 + NC, :], axis=0, keepdims=True),
         jnp.sum(st[48:48 + NC, :], axis=0, keepdims=True),
         jnp.zeros((16 - NC - 4, 128), F32)], axis=0)

    stats[0:16, :] = my_stats
    for k in range(1, 8):
        remote(stats.at[pl.ds(0, 16), :], stats.at[pl.ds(16 * k, 16), :], st_s, st_r, me ^ k).start()

    def send_rest(i, _):
        own_start(i, PIECE, B - PIECE)
        return 0

    lax.fori_loop(EARLY, NC, send_rest, 0)

    others = stats.at[pl.ds(16, 112), :]
    st_all = remote(others, others, st_s, st_r, nx)
    st_all.wait_recv()
    allst = [stats[16 * k:16 * (k + 1), :] for k in range(8)]
    top = allst[0][NC:NC + 1, :]
    for s in allst[1:]:
        top = jnp.maximum(top, s[NC:NC + 1, :])
    total = weighted = hit = jnp.zeros((1, 128), F32)
    for s in allst:
        scale = jnp.exp(s[NC:NC + 1, :] - top)
        total = total + scale * s[NC + 1:NC + 2, :]
        weighted = weighted + scale * s[NC + 2:NC + 3, :]
        hit = hit + s[NC + 3:NC + 4, :]
    log_norm = top + jnp.log(total)
    small[0:1, :] = log_norm
    small[1:2, :] = log_norm - weighted / total
    small[2:3, :] = hit - log_norm
    small[3:8, :] = jnp.zeros((5, 128), F32)
    offs[...] = jnp.transpose(stats[...] - log_norm)

    lane16 = lax.broadcasted_iota(jnp.int32, (PIECE, 128), 1)

    def fix(rel, i):
        dev = me ^ rel
        row, cols = place(dev, i)
        for k in range(8):
            rows = pl.ds(rows_of(dev ^ k), PIECE)
            off = jnp.sum(jnp.where(lane16 == rel * 16 + i, offs[rows, :], 0.0), axis=-1, keepdims=True)
            val = w[pl.ds(row + k * PIECE, PIECE), cols].astype(F32) + off
            out[rows, pl.ds(pl.multiple_of(dev * VL + i * CW, CW), CW)] = val.astype(BF16)

    def land(n):
        return w.at[pl.ds(0, n * 128), pl.ds(0, CW)]

    def arrived(n, sem):
        remote(land(n), land(n), bulk_s, sem, nx).wait_recv()

    def forward(rel, i, sem, to):
        ref = chunk(me ^ rel, i)
        remote(ref, ref, bulk_s, sem, to).start()

    def arrivals(i, _):
        arrived(2, rxy.at[i])

        @pl.when(i % 2 == 0)
        def _():
            forward(2, i, rd.at[i], ny)

        @pl.when(i % 2 == 1)
        def _():
            forward(4, i, rd.at[i], nx)

        forward(2, i, pr.at[i], pt)
        forward(4, i, pr.at[i], pt)
        fix(0, i)
        fix(2, i)
        fix(4, i)
        arrived(3, pr.at[i])
        fix(1, i)
        fix(3, i)
        fix(5, i)
        return 0

    lax.fori_loop(0, NC, arrivals, 0)

    def diagonal(i, _):
        arrived(1, rd.at[i])
        forward(6, i, prd.at[i], pt)
        fix(6, i)
        arrived(1, prd.at[i])
        fix(7, i)
        return 0

    lax.fori_loop(0, NC, diagonal, 0)

    def left(ref, sem):
        remote(ref, ref, sem, rs_r, nx).wait_send()

    left(ysend, d2d_s)
    rs_all.wait_send()
    left(xbuf.at[pl.ds(0, 7 * PIECE), :], x_s)
    st_all.wait_send()
    left(w.at[pl.ds(0, 1792), :], bulk_s)


def _write(src, small, out, o0, o1, o2, sem):
    step = B // 8
    cs = [pltpu.make_async_copy(small.at[pl.ds(k, 1), :], o, sem.at[8 + k]) for k, o in enumerate((o0, o1, o2))]
    cs += [pltpu.make_async_copy(src.at[pl.ds(k * step, step)], out.at[pl.ds(k * step, step)], sem.at[k]) for k in range(8)]
    for c in cs:
        c.start()
    for c in cs:
        c.wait()


def solution(mesh):
    vmem = pl.BlockSpec(memory_space=pltpu.VMEM)
    hbm = pl.BlockSpec(memory_space=pltpu.HBM)
    dma = pltpu.SemaphoreType.DMA

    def device_step(hidden, w_gate, w_up, w_down, norm_gain, w_vocab, temperature, target):
        wide, small = pl.pallas_call(
            _main,
            out_shape=(pltpu.VMEM((B, V), BF16), pltpu.VMEM((8, 128), F32)),
            in_specs=[hbm] * 8,
            out_specs=(vmem, vmem),
            scratch_shapes=[
                pltpu.VMEM((2048, 3072), BF16), pltpu.VMEM((D, VL), BF16), pltpu.VMEM((B, D), BF16),
                pltpu.VMEM((B, FL), BF16), pltpu.VMEM((B, D), F32), pltpu.VMEM((HALF, D), BF16),
                pltpu.VMEM((HALF, D), BF16), pltpu.VMEM((HALF, D), BF16), pltpu.VMEM((3 * PIECE, D), BF16),
                pltpu.VMEM((B, D), BF16), pltpu.VMEM((128, 128), F32), pltpu.VMEM((128, 128), F32),
                pltpu.VMEM((128, 128), F32), pltpu.VMEM((128, 128), F32), pltpu.VMEM((128, 128), jnp.int32),
                pltpu.VMEM((1, D), F32), pltpu.VMEM((1, B), F32), pltpu.VMEM((1, B), jnp.int32),
                dma((4,)), dma((NF,)), dma((NJ,)), dma((NW,)),
                dma, dma((NJ,)), dma, dma, dma, dma((3,)), dma, dma, dma, dma,
                dma((NC,)), dma((NC,)), dma((NC,)), dma((NC,)),
            ],
            compiler_params=pltpu.CompilerParams(collective_id=0, has_side_effects=True, vmem_limit_bytes=49 << 20),
            name="step",
        )(hidden, w_gate, w_up, w_down, norm_gain.reshape(1, D), w_vocab, temperature.reshape(1, B), target.reshape(1, B))
        row = jax.ShapeDtypeStruct((1, B), F32)
        log_probs, log_norm, entropy, target_logp = pl.pallas_call(
            _write,
            out_shape=(jax.ShapeDtypeStruct((B, V), BF16), row, row, row),
            in_specs=[vmem, vmem],
            out_specs=(hbm, hbm, hbm, hbm),
            scratch_shapes=[dma((11,))],
            compiler_params=pltpu.CompilerParams(vmem_limit_bytes=16 << 20),
            name="write",
        )(wide, small)
        return log_norm.reshape(B), entropy.reshape(B), target_logp.reshape(B), log_probs

    return jax.shard_map(
        device_step,
        mesh=mesh,
        in_specs=(P("dp", None), P(None, "tp"), P(None, "tp"), P("tp", None), P(None),
                  P(None, "tp"), P("dp"), P("dp")),
        out_specs=(P("dp"), P("dp"), P("dp"), P("dp", None)),
        check_vma=False,
    )
```

time: 85.5 us -> 81.2 us (0.950)
  Pallas kernels: 84.8 us -> 80.5 us
    pallas_call x1, Pallas kernels: 79.6 us -> 75.8 us  [device_step(): pl.pallas_call(_main, out_shape=(pltpu.VMEM((B, V), BF16), pltpu.VMEM((8,...]
where the time goes in v2:
time: 81.2 us; the launch traced here: 81.1 us
  Pallas kernels  80.5 us (99%)
    pallas_call x1, Pallas kernels, device_step(): pl.pallas_call(_main, out_shape=(pltpu.VMEM((B, V), BF16), pltpu.VMEM((8,...  75.8 us
    pallas_call x1, Pallas kernels, device_step(): pl.pallas_call(_write, out_shape=(jax.ShapeDtypeStruct((B, V), BF16), row...  4.7 us

profile of v2, /device:TPU:0, one launch (start us, length us, event | category | flops | bytes accessed | tf_op | source)
XLA Modules:
  0.0 81.1 jit_solution(6939944325295116496)
XLA Ops:
  0.6 75.8 %step.1 = (bf16[128,49152]{1,0:T(8,128)(2,1)S(1)}, f32[8,128]{1,0:T(8,128)S(1)}) custom-call(bf16[128,2048]{1,0:T(8,128)(2,1)} %hid_hbm.1, bf16[2048,1024]{1,0:T(8,128)(2,1)} %wg_hbm.1, bf16[2048,1024]{1,0:T(8,128)(2,1)} %wu_hbm.1, bf16[1024,2048]{1,0:T(8,128)(2,1)} %wd_hbm.1, f32[1,2048]{1,0:T(1,128)} %bitcast.6, bf16[2048,6144]{1,0:T(8,128)(2,1)} %wv_hbm.1, ...), custom_call_target="tpu_custom_call" | custom-call | tf_op jit(solution)/shard_map/step/pallas_call | solution.py:330
  76.5 4.7 %write.1 = (bf16[128,49152]{1,0:T(8,128)(2,1)}, f32[1,128]{1,0:T(1,128)}, f32[1,128]{1,0:T(1,128)}, f32[1,128]{1,0:T(1,128)}) custom-call(bf16[128,49152]{1,0:T(8,128)(2,1)S(1)} %get-tuple-element.10.src, f32[8,128]{1,0:T(8,128)S(1)} %get-tuple-element.11.small), custom_call_target="tpu_custom_call" | custom-call | tf_op jit(solution)/shard_map/write/pallas_call | solution.py:350

commit v3 on v2

--- a/solution.py
+++ b/solution.py
@@ -13,6 +13,9 @@
 CW = VL // NC
 GRID = 3072 // CW
 EARLY = 3
+OWN = 5
+SPLIT = 6
+NS = 2
 NF = 4
 FW = FL // NF
 NJ = 2
@@ -74,6 +77,8 @@
             load_wf(b + 2)
         else:
             wd_copies.append(load_wd(b - NF + 2))
+            if b == NF - 1:
+                wv_copies.append(load_wv(0))
         g = jnp.dot(hid[...], w[:, b * FW:(b + 1) * FW], preferred_element_type=F32)
         u = jnp.dot(hid[...], w[:, FL + b * FW:FL + (b + 1) * FW], preferred_element_type=F32)
         act[:, b * FW:(b + 1) * FW] = (jax.nn.silu(g) * u).astype(BF16)
@@ -84,7 +89,7 @@
     for j in range(NJ):
         cols = pl.ds(j * JW, JW)
         wd_copies[j].wait()
-        wv_copies.append(load_wv(j))
+        wv_copies.append(load_wv(j + 1))
         yf[:, j * JW:(j + 1) * JW] = jnp.dot(act[...], w[j * FL:(j + 1) * FL, 2 * FL:2 * FL + JW], preferred_element_type=F32)
         ysend[:, j * JW:(j + 1) * JW] = yf[pl.ds(give, HALF), j * JW:(j + 1) * JW].astype(BF16)
         if j == 0:
@@ -96,6 +101,8 @@
     def rows_of(dev):
         return pl.multiple_of((dev % 2) * HALF + (dev // 2) * PIECE, PIECE)
 
+    for n in range(NJ + 1, NW):
+        wv_copies.append(load_wv(n))
     for c in small_copies:
         c.wait()
     offs[...] = _lanes(1.0 / temp[...])
@@ -117,9 +124,6 @@
         for s, dev in enumerate((nd, nx, ny)):
             remote(psend.at[pl.ds(piece(dev), PIECE), pl.ds(j * JW, JW)], precv.at[pl.ds(s * PIECE, PIECE), pl.ds(j * JW, JW)],
                    rs_s, rs_r, dev).start()
-    for n in range(NJ, NW):
-        wv_copies.append(load_wv(n))
-
     rs_all = remote(precv, precv, rs_s, rs_r, nx)
     rs_all.wait_recv()
     mine = rows_of(me)
@@ -164,9 +168,9 @@
         row, _ = place(me, i)
         for q, p in enumerate(parts):
             w[pl.ds(row + first, count), pl.ds(pl.multiple_of((i % GRID) * CW + q * 128, 128), 128)] = (p - top).astype(BF16)
-        if first == 0:
+        if count == PIECE:
             own_start(i, first, count)
-        else:
+        elif first:
             @pl.when(i < EARLY)
             def _():
                 own_start(i, first, count)
@@ -194,15 +198,25 @@
         head(i, PIECE, B - PIECE)
         return 0
 
-    for c in wv_copies:
-        c.wait()
-    lax.fori_loop(0, NC, head_own, 0)
+    def head_all(i, _):
+        head(i, 0, B)
+        return 0
+
+    ready = 0
+    for i in range(OWN):
+        while ready * WW < (i + 1) * CW:
+            wv_copies[ready].wait()
+            ready += 1
+        head_own(i, 0)
     for s, k in ((1, 2), (2, 4), (0, 6)):
         remote(xrow(k), xrow(k), x_s, xa_r.at[s], me ^ k).wait_recv()
         remote(xrow(k), xrow(k + 1), x_s, xf_r, pt).start()
     four = xbuf.at[pl.ds(0, 4 * PIECE), :]
     remote(four, four, x_s, xf_r, pt).wait_recv()
-    lax.fori_loop(0, NC, head_rest, 0)
+    for c in wv_copies[ready:]:
+        c.wait()
+    lax.fori_loop(0, OWN, head_rest, 0)
+    lax.fori_loop(OWN, NC, head_all, 0)
 
     for k in range(8):
         offs[pl.ds(rows_of(me ^ k), PIECE), :] = statm[k * PIECE:(k + 1) * PIECE, :]
@@ -224,7 +238,12 @@
         own_start(i, PIECE, B - PIECE)
         return 0
 
-    lax.fori_loop(EARLY, NC, send_rest, 0)
+    def send_all(i, _):
+        own_start(i, 0, B)
+        return 0
+
+    lax.fori_loop(EARLY, OWN, send_rest, 0)
+    lax.fori_loop(OWN, NC, send_all, 0)
 
     others = stats.at[pl.ds(16, 112), :]
     st_all = remote(others, others, st_s, st_r, nx)
@@ -248,10 +267,10 @@
 
     lane16 = lax.broadcasted_iota(jnp.int32, (PIECE, 128), 1)
 
-    def fix(rel, i):
+    def fix(rel, i, first=0, count=8):
         dev = me ^ rel
         row, cols = place(dev, i)
-        for k in range(8):
+        for k in range(first, first + count):
             rows = pl.ds(rows_of(dev ^ k), PIECE)
             off = jnp.sum(jnp.where(lane16 == rel * 16 + i, offs[rows, :], 0.0), axis=-1, keepdims=True)
             val = w[pl.ds(row + k * PIECE, PIECE), cols].astype(F32) + off
@@ -267,16 +286,33 @@
         ref = chunk(me ^ rel, i)
         remote(ref, ref, bulk_s, sem, to).start()
 
+    def pieces(rel, i, n):
+        row, cols = place(me ^ rel, i)
+        return w.at[pl.ds(row + n * (128 // NS), 128 // NS), cols]
+
+    def piece_sem(sems, i, n):
+        return sems.at[i if n == 0 else NC + (i - SPLIT) * (NS - 1) + n - 1]
+
+    def relay(rel, i, to):
+        if isinstance(i, int):
+            for n in range(NS):
+                ref = pieces(rel, i, n)
+                remote(ref, ref, bulk_s, piece_sem(rd, i, n), to).start()
+        else:
+            forward(rel, i, rd.at[i], to)
+
     def arrivals(i, _):
         arrived(2, rxy.at[i])
-
-        @pl.when(i % 2 == 0)
-        def _():
-            forward(2, i, rd.at[i], ny)
-
-        @pl.when(i % 2 == 1)
-        def _():
-            forward(4, i, rd.at[i], nx)
+        if isinstance(i, int):
+            relay(2, i, ny) if i % 2 == 0 else relay(4, i, nx)
+        else:
+            @pl.when(i % 2 == 0)
+            def _():
+                relay(2, i, ny)
+
+            @pl.when(i % 2 == 1)
+            def _():
+                relay(4, i, nx)
 
         forward(2, i, pr.at[i], pt)
         forward(4, i, pr.at[i], pt)
@@ -289,7 +325,9 @@
         fix(5, i)
         return 0
 
-    lax.fori_loop(0, NC, arrivals, 0)
+    lax.fori_loop(0, SPLIT, arrivals, 0)
+    for i in range(SPLIT, NC):
+        arrivals(i, 0)
 
     def diagonal(i, _):
         arrived(1, rd.at[i])
@@ -299,7 +337,18 @@
         fix(7, i)
         return 0
 
-    lax.fori_loop(0, NC, diagonal, 0)
+    lax.fori_loop(0, SPLIT, diagonal, 0)
+    quarter = w.at[pl.ds(0, 128 // NS), pl.ds(0, CW)]
+    for n in range(NS):
+        for i in range(SPLIT, NC):
+            remote(quarter, quarter, bulk_s, piece_sem(rd, i, n), nx).wait_recv()
+            ref = pieces(6, i, n)
+            remote(ref, ref, bulk_s, piece_sem(prd, i, n), pt).start()
+            fix(6, i, 8 // NS * n, 8 // NS)
+    for n in range(NS):
+        for i in range(SPLIT, NC):
+            remote(quarter, quarter, bulk_s, piece_sem(prd, i, n), pt).wait_recv()
+            fix(7, i, 8 // NS * n, 8 // NS)
 
     def left(ref, sem):
         remote(ref, ref, sem, rs_r, nx).wait_send()
@@ -341,7 +390,7 @@
                 pltpu.VMEM((1, D), F32), pltpu.VMEM((1, B), F32), pltpu.VMEM((1, B), jnp.int32),
                 dma((4,)), dma((NF,)), dma((NJ,)), dma((NW,)),
                 dma, dma((NJ,)), dma, dma, dma, dma((3,)), dma, dma, dma, dma,
-                dma((NC,)), dma((NC,)), dma((NC,)), dma((NC,)),
+                dma((NC,)), dma((NC + (NC - SPLIT) * (NS - 1),)), dma((NC,)), dma((NC + (NC - SPLIT) * (NS - 1),)),
             ],
             compiler_params=pltpu.CompilerParams(collective_id=0, has_side_effects=True, vmem_limit_bytes=49 << 20),
             name="step",

time: 81.2 us -> 78.6 us (0.968)
  Pallas kernels: 80.5 us -> 77.8 us
    pallas_call x1, Pallas kernels: 75.8 us -> 73.1 us  [device_step(): pl.pallas_call(_main, out_shape=(pltpu.VMEM((B, V), BF16), pltpu.VMEM((8,...]
where the time goes in v3:
time: 78.6 us; the launch traced here: 78.5 us
  Pallas kernels  77.8 us (99%)
    pallas_call x1, Pallas kernels, device_step(): pl.pallas_call(_main, out_shape=(pltpu.VMEM((B, V), BF16), pltpu.VMEM((8,...  73.1 us
    pallas_call x1, Pallas kernels, device_step(): pl.pallas_call(_write, out_shape=(jax.ShapeDtypeStruct((B, V), BF16), row...  4.7 us

profile of v3, /device:TPU:0, one launch (start us, length us, event | category | flops | bytes accessed | tf_op | source)
XLA Modules:
  0.0 78.5 jit_solution(3830570655103938108)
XLA Ops:
  0.6 73.1 %step.1 = (bf16[128,49152]{1,0:T(8,128)(2,1)S(1)}, f32[8,128]{1,0:T(8,128)S(1)}) custom-call(bf16[128,2048]{1,0:T(8,128)(2,1)} %hid_hbm.1, bf16[2048,1024]{1,0:T(8,128)(2,1)} %wg_hbm.1, bf16[2048,1024]{1,0:T(8,128)(2,1)} %wu_hbm.1, bf16[1024,2048]{1,0:T(8,128)(2,1)} %wd_hbm.1, f32[1,2048]{1,0:T(1,128)} %bitcast.6, bf16[2048,6144]{1,0:T(8,128)(2,1)} %wv_hbm.1, ...), custom_call_target="tpu_custom_call" | custom-call | tf_op jit(solution)/shard_map/step/pallas_call | solution.py:379
  73.8 4.7 %write.1 = (bf16[128,49152]{1,0:T(8,128)(2,1)}, f32[1,128]{1,0:T(1,128)}, f32[1,128]{1,0:T(1,128)}, f32[1,128]{1,0:T(1,128)}) custom-call(bf16[128,49152]{1,0:T(8,128)(2,1)S(1)} %get-tuple-element.10.src, f32[8,128]{1,0:T(8,128)S(1)} %get-tuple-element.11.small), custom_call_target="tpu_custom_call" | custom-call | tf_op jit(solution)/shard_map/write/pallas_call | solution.py:399

commit v4 on v3

--- a/solution.py
+++ b/solution.py
@@ -13,16 +13,21 @@
 CW = VL // NC
 GRID = 3072 // CW
 EARLY = 3
-OWN = 5
+OWN = 6
 SPLIT = 6
-NS = 2
+CUTS = (0, 4, 7, 8)
+NS = len(CUTS) - 1
 NF = 4
 FW = FL // NF
-NJ = 2
+NJ = 4
 JW = D // NJ
 HALF, PIECE = 64, 16
 NW = 4
 WW = VL // NW
+
+
+ORDER = (0, 2, 4, 6, 1, 3, 5, 7)
+POS = tuple(ORDER.index(k) for k in range(8))
 
 
 def _lanes(row):
@@ -55,7 +60,7 @@
         pltpu.make_async_copy(wv_hbm.at[:, pl.ds(0, 2 * FW)], both, wf_sem.at[b]).wait()
 
     def load_wd(j):
-        return load(wd_hbm.at[:, pl.ds(j * JW, JW)], w.at[pl.ds(j * FL, FL), pl.ds(2 * FL, JW)], wd_sem.at[j])
+        return load(wd_hbm.at[:, pl.ds(j * JW, JW)], w.at[pl.ds(j % 2 * FL, FL), pl.ds(2 * FL + j // 2 * JW, JW)], wd_sem.at[j])
 
     def load_wv(n):
         return load(wv_hbm.at[:, pl.ds(n * WW, WW)], wv.at[:, pl.ds(n * WW, WW)], wv_sem.at[n])
@@ -76,7 +81,8 @@
         if b < NF - 2:
             load_wf(b + 2)
         else:
-            wd_copies.append(load_wd(b - NF + 2))
+            for j in range((b - NF + 2) * NJ // 2, (b - NF + 3) * NJ // 2):
+                wd_copies.append(load_wd(j))
             if b == NF - 1:
                 wv_copies.append(load_wv(0))
         g = jnp.dot(hid[...], w[:, b * FW:(b + 1) * FW], preferred_element_type=F32)
@@ -89,8 +95,10 @@
     for j in range(NJ):
         cols = pl.ds(j * JW, JW)
         wd_copies[j].wait()
-        wv_copies.append(load_wv(j + 1))
-        yf[:, j * JW:(j + 1) * JW] = jnp.dot(act[...], w[j * FL:(j + 1) * FL, 2 * FL:2 * FL + JW], preferred_element_type=F32)
+        if j < NW - 1:
+            wv_copies.append(load_wv(j + 1))
+        wd = w[j % 2 * FL:(j % 2 + 1) * FL, 2 * FL + j // 2 * JW:2 * FL + (j // 2 + 1) * JW]
+        yf[:, j * JW:(j + 1) * JW] = jnp.dot(act[...], wd, preferred_element_type=F32)
         ysend[:, j * JW:(j + 1) * JW] = yf[pl.ds(give, HALF), j * JW:(j + 1) * JW].astype(BF16)
         if j == 0:
             pl.semaphore_wait(barrier, 7)
@@ -101,16 +109,16 @@
     def rows_of(dev):
         return pl.multiple_of((dev % 2) * HALF + (dev // 2) * PIECE, PIECE)
 
-    for n in range(NJ + 1, NW):
+    for n in range(min(NJ + 1, NW), NW):
         wv_copies.append(load_wv(n))
     for c in small_copies:
         c.wait()
     offs[...] = _lanes(1.0 / temp[...])
     statm[...] = _lanes(tgt[...].astype(F32))
-    for k in range(8):
+    for p, k in enumerate(ORDER):
         rows = pl.ds(rows_of(me ^ k), PIECE)
-        invt[k * PIECE:(k + 1) * PIECE, :] = offs[rows, :]
-        tgtm[k * PIECE:(k + 1) * PIECE, :] = statm[rows, :].astype(jnp.int32)
+        invt[p * PIECE:(p + 1) * PIECE, :] = offs[rows, :]
+        tgtm[p * PIECE:(p + 1) * PIECE, :] = statm[rows, :].astype(jnp.int32)
 
     def piece(dev):
         return pl.multiple_of((dev // 2) * PIECE, PIECE)
@@ -135,7 +143,7 @@
     xbuf[0:PIECE, :] = (gain[...] * res * inv_rms).astype(BF16)
 
     def xrow(k):
-        return xbuf.at[pl.ds(k * PIECE, PIECE), :]
+        return xbuf.at[pl.ds(POS[k] * PIECE, PIECE), :]
 
     for s, k in enumerate((6, 2, 4)):
         remote(xrow(0), xrow(k), x_s, xa_r.at[s], me ^ k).start()
@@ -157,7 +165,7 @@
         remote(ref, ref, bulk_s, rxy.at[i], ny).start()
         remote(ref, ref, bulk_s, pr.at[i], pt).start()
 
-    def head(i, first, count):
+    def head(i, first, count, go=False):
         acc = jnp.dot(xbuf[first:first + count, :], wv[:, pl.ds(pl.multiple_of(i * CW, CW), CW)], preferred_element_type=F32)
         scale = invt[first:first + count, :]
         parts = [acc[:, q * 128:(q + 1) * 128] * scale for q in range(CW // 128)]
@@ -168,7 +176,7 @@
         row, _ = place(me, i)
         for q, p in enumerate(parts):
             w[pl.ds(row + first, count), pl.ds(pl.multiple_of((i % GRID) * CW + q * 128, 128), 128)] = (p - top).astype(BF16)
-        if count == PIECE:
+        if go:
             own_start(i, first, count)
         elif first:
             @pl.when(i < EARLY)
@@ -191,7 +199,7 @@
         statm[first:first + count, :] = sm
 
     def head_own(i, _):
-        head(i, 0, PIECE)
+        head(i, 0, PIECE, True)
         return 0
 
     def head_rest(i, _):
@@ -211,15 +219,17 @@
     for s, k in ((1, 2), (2, 4), (0, 6)):
         remote(xrow(k), xrow(k), x_s, xa_r.at[s], me ^ k).wait_recv()
         remote(xrow(k), xrow(k + 1), x_s, xf_r, pt).start()
+    head(0, PIECE, HALF - PIECE, True)
     four = xbuf.at[pl.ds(0, 4 * PIECE), :]
     remote(four, four, x_s, xf_r, pt).wait_recv()
+    head(0, HALF, HALF, True)
     for c in wv_copies[ready:]:
         c.wait()
-    lax.fori_loop(0, OWN, head_rest, 0)
+    lax.fori_loop(1, OWN, head_rest, 0)
     lax.fori_loop(OWN, NC, head_all, 0)
 
-    for k in range(8):
-        offs[pl.ds(rows_of(me ^ k), PIECE), :] = statm[k * PIECE:(k + 1) * PIECE, :]
+    for p, k in enumerate(ORDER):
+        offs[pl.ds(rows_of(me ^ k), PIECE), :] = statm[p * PIECE:(p + 1) * PIECE, :]
     st = jnp.transpose(offs[...])
     tops = st[0:NC, :]
     top = jnp.max(tops, axis=0, keepdims=True)
@@ -271,7 +281,7 @@
         dev = me ^ rel
         row, cols = place(dev, i)
         for k in range(first, first + count):
-            rows = pl.ds(rows_of(dev ^ k), PIECE)
+            rows = pl.ds(rows_of(dev ^ ORDER[k]), PIECE)
             off = jnp.sum(jnp.where(lane16 == rel * 16 + i, offs[rows, :], 0.0), axis=-1, keepdims=True)
             val = w[pl.ds(row + k * PIECE, PIECE), cols].astype(F32) + off
             out[rows, pl.ds(pl.multiple_of(dev * VL + i * CW, CW), CW)] = val.astype(BF16)
@@ -288,7 +298,7 @@
 
     def pieces(rel, i, n):
         row, cols = place(me ^ rel, i)
-        return w.at[pl.ds(row + n * (128 // NS), 128 // NS), cols]
+        return w.at[pl.ds(row + CUTS[n] * PIECE, (CUTS[n + 1] - CUTS[n]) * PIECE), cols]
 
     def piece_sem(sems, i, n):
         return sems.at[i if n == 0 else NC + (i - SPLIT) * (NS - 1) + n - 1]
@@ -298,6 +308,7 @@
             for n in range(NS):
                 ref = pieces(rel, i, n)
                 remote(ref, ref, bulk_s, piece_sem(rd, i, n), to).start()
+            remote(ref, ref, bulk_s, piece_sem(prd, i, NS - 1), to ^ 1).start()
         else:
             forward(rel, i, rd.at[i], to)
 
@@ -338,17 +349,20 @@
         return 0
 
     lax.fori_loop(0, SPLIT, diagonal, 0)
-    quarter = w.at[pl.ds(0, 128 // NS), pl.ds(0, CW)]
+    def part(n):
+        return w.at[pl.ds(0, (CUTS[n + 1] - CUTS[n]) * PIECE), pl.ds(0, CW)]
+
     for n in range(NS):
         for i in range(SPLIT, NC):
-            remote(quarter, quarter, bulk_s, piece_sem(rd, i, n), nx).wait_recv()
-            ref = pieces(6, i, n)
-            remote(ref, ref, bulk_s, piece_sem(prd, i, n), pt).start()
-            fix(6, i, 8 // NS * n, 8 // NS)
+            remote(part(n), part(n), bulk_s, piece_sem(rd, i, n), nx).wait_recv()
+            if n < NS - 1:
+                ref = pieces(6, i, n)
+                remote(ref, ref, bulk_s, piece_sem(prd, i, n), pt).start()
+            fix(6, i, CUTS[n], CUTS[n + 1] - CUTS[n])
     for n in range(NS):
         for i in range(SPLIT, NC):
-            remote(quarter, quarter, bulk_s, piece_sem(prd, i, n), pt).wait_recv()
-            fix(7, i, 8 // NS * n, 8 // NS)
+            remote(part(n), part(n), bulk_s, piece_sem(prd, i, n), pt).wait_recv()
+            fix(7, i, CUTS[n], CUTS[n + 1] - CUTS[n])
 
     def left(ref, sem):
         remote(ref, ref, sem, rs_r, nx).wait_send()
@@ -361,13 +375,15 @@
 
 
 def _write(src, small, out, o0, o1, o2, sem):
-    step = B // 8
-    cs = [pltpu.make_async_copy(small.at[pl.ds(k, 1), :], o, sem.at[8 + k]) for k, o in enumerate((o0, o1, o2))]
-    cs += [pltpu.make_async_copy(src.at[pl.ds(k * step, step)], out.at[pl.ds(k * step, step)], sem.at[k]) for k in range(8)]
+    step = B // 16
+    cs = [pltpu.make_async_copy(small.at[pl.ds(k, 1), :], o, sem.at[k]) for k, o in enumerate((o0, o1, o2))]
+    for k in range(16):
+        pltpu.make_async_copy(src.at[pl.ds(k * step, step)], out.at[pl.ds(k * step, step)], sem.at[3]).start()
     for c in cs:
         c.start()
     for c in cs:
         c.wait()
+    pltpu.make_async_copy(src, out, sem.at[3]).wait()
 
 
 def solution(mesh):
@@ -401,7 +417,7 @@
             out_shape=(jax.ShapeDtypeStruct((B, V), BF16), row, row, row),
             in_specs=[vmem, vmem],
             out_specs=(hbm, hbm, hbm, hbm),
-            scratch_shapes=[dma((11,))],
+            scratch_shapes=[dma((4,))],
             compiler_params=pltpu.CompilerParams(vmem_limit_bytes=16 << 20),
             name="write",
         )(wide, small)

time: 78.6 us -> 76.6 us (0.975)
  Pallas kernels: 77.8 us -> 75.9 us
    pallas_call x1, Pallas kernels: 73.1 us -> 71.3 us  [device_step(): pl.pallas_call(_main, out_shape=(pltpu.VMEM((B, V), BF16), pltpu.VMEM((8,...]
where the time goes in v4:
time: 76.6 us; the launch traced here: 76.5 us
  Pallas kernels  75.9 us (99%)
    pallas_call x1, Pallas kernels, device_step(): pl.pallas_call(_main, out_shape=(pltpu.VMEM((B, V), BF16), pltpu.VMEM((8,...  71.3 us
    pallas_call x1, Pallas kernels, device_step(): pl.pallas_call(_write, out_shape=(jax.ShapeDtypeStruct((B, V), BF16), row...  4.6 us

profile of v4, /device:TPU:0, one launch (start us, length us, event | category | flops | bytes accessed | tf_op | source)
XLA Modules:
  0.0 76.5 jit_solution(14476194887905630895)
XLA Ops:
  0.6 71.3 %step.1 = (bf16[128,49152]{1,0:T(8,128)(2,1)S(1)}, f32[8,128]{1,0:T(8,128)S(1)}) custom-call(bf16[128,2048]{1,0:T(8,128)(2,1)} %hid_hbm.1, bf16[2048,1024]{1,0:T(8,128)(2,1)} %wg_hbm.1, bf16[2048,1024]{1,0:T(8,128)(2,1)} %wu_hbm.1, bf16[1024,2048]{1,0:T(8,128)(2,1)} %wd_hbm.1, f32[1,2048]{1,0:T(1,128)} %bitcast.6, bf16[2048,6144]{1,0:T(8,128)(2,1)} %wv_hbm.1, ...), custom_call_target="tpu_custom_call" | custom-call | tf_op jit(solution)/shard_map/step/pallas_call | solution.py:395
  72.0 4.6 %write.1 = (bf16[128,49152]{1,0:T(8,128)(2,1)}, f32[1,128]{1,0:T(1,128)}, f32[1,128]{1,0:T(1,128)}, f32[1,128]{1,0:T(1,128)}) custom-call(bf16[128,49152]{1,0:T(8,128)(2,1)S(1)} %get-tuple-element.10.src, f32[8,128]{1,0:T(8,128)S(1)} %get-tuple-element.11.small), custom_call_target="tpu_custom_call" | custom-call | tf_op jit(solution)/shard_map/write/pallas_call | solution.py:415

commit v5 on v4

--- a/solution.py
+++ b/solution.py
@@ -13,7 +13,8 @@
 CW = VL // NC
 GRID = 3072 // CW
 EARLY = 3
-OWN = 6
+OWN = 7
+GROUP = 2
 SPLIT = 6
 CUTS = (0, 4, 7, 8)
 NS = len(CUTS) - 1
@@ -36,7 +37,7 @@
 
 def _main(hid_hbm, wg_hbm, wu_hbm, wd_hbm, gain_hbm, wv_hbm, temp_hbm, tgt_hbm,
           out, small,
-          w, wv, hid, act, yf, ysend, yrecv, psend, precv, xbuf, statm, stats, offs, invt, tgtm, gain, temp, tgt,
+          w, wv, hid, act, yf, yall, ysend, yrecv, psend, precv0, precv, xbuf, kept, statm, stats, offs, invt, tgtm, gain, temp, tgt,
           in_sem, wf_sem, wd_sem, wv_sem,
           d2d_s, d2d_r, rs_s, rs_r, x_s, xa_r, xf_r, st_s, st_r, bulk_s, rxy, rd, pr, prd):
     me = lax.axis_index("tp")
@@ -89,25 +90,30 @@
         u = jnp.dot(hid[...], w[:, FL + b * FW:FL + (b + 1) * FW], preferred_element_type=F32)
         act[:, b * FW:(b + 1) * FW] = (jax.nn.silu(g) * u).astype(BF16)
 
+    def rows_of(dev):
+        return pl.multiple_of((dev % 2) * HALF + (dev // 2) * PIECE, PIECE)
+
     keep = pl.multiple_of(core * HALF, HALF)
     give = pl.multiple_of(HALF - core * HALF, HALF)
     d2d = []
     for j in range(NJ):
-        cols = pl.ds(j * JW, JW)
         wd_copies[j].wait()
         if j < NW - 1:
             wv_copies.append(load_wv(j + 1))
         wd = w[j % 2 * FL:(j % 2 + 1) * FL, 2 * FL + j // 2 * JW:2 * FL + (j // 2 + 1) * JW]
         yf[:, j * JW:(j + 1) * JW] = jnp.dot(act[...], wd, preferred_element_type=F32)
-        ysend[:, j * JW:(j + 1) * JW] = yf[pl.ds(give, HALF), j * JW:(j + 1) * JW].astype(BF16)
         if j == 0:
+            yall[...] = yf[:, 0:JW].astype(BF16)
             pl.semaphore_wait(barrier, 7)
-        c = remote(ysend.at[:, cols], yrecv.at[:, cols], d2d_s, d2d_r.at[j], pt)
+            for k in (6, 7, 2, 3, 4, 5, 1):
+                remote(yall.at[pl.ds(rows_of(me ^ k), PIECE), :], precv0.at[pl.ds((k - 1) * PIECE, PIECE), :],
+                       rs_s, rs_r, me ^ k).start()
+            continue
+        ysend[:, (j - 1) * JW:j * JW] = yf[pl.ds(give, HALF), j * JW:(j + 1) * JW].astype(BF16)
+        cols = pl.ds((j - 1) * JW, JW)
+        c = remote(ysend.at[:, cols], yrecv.at[:, cols], d2d_s, d2d_r.at[j - 1], pt)
         c.start()
         d2d.append(c)
-
-    def rows_of(dev):
-        return pl.multiple_of((dev % 2) * HALF + (dev // 2) * PIECE, PIECE)
 
     for n in range(min(NJ + 1, NW), NW):
         wv_copies.append(load_wv(n))
@@ -123,21 +129,26 @@
     def piece(dev):
         return pl.multiple_of((dev // 2) * PIECE, PIECE)
 
-    for j in range(NJ):
+    for j in range(1, NJ):
         cols = slice(j * JW, (j + 1) * JW)
-        d2d[j].wait_recv()
-        part = yf[pl.ds(keep, HALF), cols] + yrecv[:, cols].astype(F32)
+        got = pl.ds((j - 1) * JW, JW)
+        d2d[j - 1].wait_recv()
+        part = yf[pl.ds(keep, HALF), cols] + yrecv[:, (j - 1) * JW:j * JW].astype(F32)
         yf[pl.ds(keep, HALF), cols] = part
-        psend[:, cols] = part.astype(BF16)
+        psend[:, (j - 1) * JW:j * JW] = part.astype(BF16)
         for s, dev in enumerate((nd, nx, ny)):
-            remote(psend.at[pl.ds(piece(dev), PIECE), pl.ds(j * JW, JW)], precv.at[pl.ds(s * PIECE, PIECE), pl.ds(j * JW, JW)],
-                   rs_s, rs_r, dev).start()
-    rs_all = remote(precv, precv, rs_s, rs_r, nx)
+            remote(psend.at[pl.ds(piece(dev), PIECE), got], precv.at[pl.ds(s * PIECE, PIECE), got], rs_s, rs_r, dev).start()
+
+    rs_all = remote(hid.at[pl.ds(0, HALF), :], hid.at[pl.ds(0, HALF), :], rs_s, rs_r, nx)
     rs_all.wait_recv()
     mine = rows_of(me)
-    y = yf[pl.ds(mine, PIECE), :]
+    y0 = yf[pl.ds(mine, PIECE), 0:JW]
+    for k in range(7):
+        y0 = y0 + precv0[k * PIECE:(k + 1) * PIECE, :].astype(F32)
+    y1 = yf[pl.ds(mine, PIECE), JW:D]
     for s in range(3):
-        y = y + precv[s * PIECE:(s + 1) * PIECE, :].astype(F32)
+        y1 = y1 + precv[s * PIECE:(s + 1) * PIECE, :].astype(F32)
+    y = jnp.concatenate([y0, y1], axis=-1)
     res = hid[pl.ds(mine, PIECE), :].astype(F32) + y
     inv_rms = lax.rsqrt(jnp.mean(res * res, axis=-1, keepdims=True) + NORM_EPS)
     xbuf[0:PIECE, :] = (gain[...] * res * inv_rms).astype(BF16)
@@ -165,24 +176,23 @@
         remote(ref, ref, bulk_s, rxy.at[i], ny).start()
         remote(ref, ref, bulk_s, pr.at[i], pt).start()
 
-    def head(i, first, count, go=False):
+    def logits(i, first, count):
         acc = jnp.dot(xbuf[first:first + count, :], wv[:, pl.ds(pl.multiple_of(i * CW, CW), CW)], preferred_element_type=F32)
         scale = invt[first:first + count, :]
-        parts = [acc[:, q * 128:(q + 1) * 128] * scale for q in range(CW // 128)]
+        return [acc[:, q * 128:(q + 1) * 128] * scale for q in range(CW // 128)]
+
+    def row_max(parts):
         top = parts[0]
         for p in parts[1:]:
             top = jnp.maximum(top, p)
-        top = jnp.max(top, axis=-1, keepdims=True)
+        return jnp.max(top, axis=-1, keepdims=True)
+
+    def put(i, first, count, parts, top):
         row, _ = place(me, i)
         for q, p in enumerate(parts):
             w[pl.ds(row + first, count), pl.ds(pl.multiple_of((i % GRID) * CW + q * 128, 128), 128)] = (p - top).astype(BF16)
-        if go:
-            own_start(i, first, count)
-        elif first:
-            @pl.when(i < EARLY)
-            def _():
-                own_start(i, first, count)
-
+
+    def statistics(i, first, count, parts, top):
         total = weighted = hit = jnp.zeros((count, 128), F32)
         lane = lax.broadcasted_iota(jnp.int32, (count, 128), 1)
         ids = tgtm[first:first + count, :] - (me * VL + i * CW)
@@ -198,9 +208,18 @@
         sm = jnp.where(lane == 48 + i, jnp.sum(hit, axis=-1, keepdims=True), sm)
         statm[first:first + count, :] = sm
 
-    def head_own(i, _):
-        head(i, 0, PIECE, True)
-        return 0
+    def head(i, first, count, go=False):
+        parts = logits(i, first, count)
+        top = row_max(parts)
+        put(i, first, count, parts, top)
+        if go:
+            own_start(i, first, count)
+        elif first:
+            @pl.when(i < EARLY)
+            def _():
+                own_start(i, first, count)
+
+        statistics(i, first, count, parts, top)
 
     def head_rest(i, _):
         head(i, PIECE, B - PIECE)
@@ -210,12 +229,24 @@
         head(i, 0, B)
         return 0
 
+    def own_statistics(i, _):
+        parts = [kept[:, pl.ds(pl.multiple_of(i * CW + q * 128, 128), 128)] for q in range(CW // 128)]
+        statistics(i, 0, PIECE, parts, row_max(parts))
+        return 0
+
     ready = 0
-    for i in range(OWN):
-        while ready * WW < (i + 1) * CW:
+    for start in range(0, OWN, GROUP):
+        group = range(start, min(start + GROUP, OWN))
+        while ready * WW < (group[-1] + 1) * CW:
             wv_copies[ready].wait()
             ready += 1
-        head_own(i, 0)
+        block = [logits(i, 0, PIECE) for i in group]
+        for i, parts in zip(group, block):
+            put(i, 0, PIECE, parts, row_max(parts))
+            for q, p in enumerate(parts):
+                kept[:, i * CW + q * 128:i * CW + (q + 1) * 128] = p
+        for i in group:
+            own_start(i, 0, PIECE)
     for s, k in ((1, 2), (2, 4), (0, 6)):
         remote(xrow(k), xrow(k), x_s, xa_r.at[s], me ^ k).wait_recv()
         remote(xrow(k), xrow(k + 1), x_s, xf_r, pt).start()
@@ -227,6 +258,7 @@
         c.wait()
     lax.fori_loop(1, OWN, head_rest, 0)
     lax.fori_loop(OWN, NC, head_all, 0)
+    lax.fori_loop(0, OWN, own_statistics, 0)
 
     for p, k in enumerate(ORDER):
         offs[pl.ds(rows_of(me ^ k), PIECE), :] = statm[p * PIECE:(p + 1) * PIECE, :]
@@ -399,13 +431,14 @@
             out_specs=(vmem, vmem),
             scratch_shapes=[
                 pltpu.VMEM((2048, 3072), BF16), pltpu.VMEM((D, VL), BF16), pltpu.VMEM((B, D), BF16),
-                pltpu.VMEM((B, FL), BF16), pltpu.VMEM((B, D), F32), pltpu.VMEM((HALF, D), BF16),
-                pltpu.VMEM((HALF, D), BF16), pltpu.VMEM((HALF, D), BF16), pltpu.VMEM((3 * PIECE, D), BF16),
-                pltpu.VMEM((B, D), BF16), pltpu.VMEM((128, 128), F32), pltpu.VMEM((128, 128), F32),
+                pltpu.VMEM((B, FL), BF16), pltpu.VMEM((B, D), F32), pltpu.VMEM((B, JW), BF16), pltpu.VMEM((HALF, D - JW), BF16),
+                pltpu.VMEM((HALF, D - JW), BF16), pltpu.VMEM((HALF, D - JW), BF16), pltpu.VMEM((7 * PIECE, JW), BF16),
+                pltpu.VMEM((3 * PIECE, D - JW), BF16),
+                pltpu.VMEM((B, D), BF16), pltpu.VMEM((PIECE, OWN * CW), F32), pltpu.VMEM((128, 128), F32), pltpu.VMEM((128, 128), F32),
                 pltpu.VMEM((128, 128), F32), pltpu.VMEM((128, 128), F32), pltpu.VMEM((128, 128), jnp.int32),
                 pltpu.VMEM((1, D), F32), pltpu.VMEM((1, B), F32), pltpu.VMEM((1, B), jnp.int32),
                 dma((4,)), dma((NF,)), dma((NJ,)), dma((NW,)),
-                dma, dma((NJ,)), dma, dma, dma, dma((3,)), dma, dma, dma, dma,
+                dma, dma((NJ - 1,)), dma, dma, dma, dma((3,)), dma, dma, dma, dma,
                 dma((NC,)), dma((NC + (NC - SPLIT) * (NS - 1),)), dma((NC,)), dma((NC + (NC - SPLIT) * (NS - 1),)),
             ],
             compiler_params=pltpu.CompilerParams(collective_id=0, has_side_effects=True, vmem_limit_bytes=49 << 20),

time: 76.6 us -> 76.4 us (level)
  no operation moved by 1% of the time
where the time goes in v5:
time: 76.4 us; the launch traced here: 76.3 us
  Pallas kernels  75.7 us (99%)
    pallas_call x1, Pallas kernels, device_step(): pl.pallas_call(_main, out_shape=(pltpu.VMEM((B, V), BF16), pltpu.VMEM((8,...  71.1 us
    pallas_call x1, Pallas kernels, device_step(): pl.pallas_call(_write, out_shape=(jax.ShapeDtypeStruct((B, V), BF16), row...  4.6 us

profile of v5, /device:TPU:0, one launch (start us, length us, event | category | flops | bytes accessed | tf_op | source)
XLA Modules:
  0.0 76.3 jit_solution(2597629485383670092)
XLA Ops:
  0.6 71.1 %step.1 = (bf16[128,49152]{1,0:T(8,128)(2,1)S(1)}, f32[8,128]{1,0:T(8,128)S(1)}) custom-call(bf16[128,2048]{1,0:T(8,128)(2,1)} %hid_hbm.1, bf16[2048,1024]{1,0:T(8,128)(2,1)} %wg_hbm.1, bf16[2048,1024]{1,0:T(8,128)(2,1)} %wu_hbm.1, bf16[1024,2048]{1,0:T(8,128)(2,1)} %wd_hbm.1, f32[1,2048]{1,0:T(1,128)} %bitcast.6, bf16[2048,6144]{1,0:T(8,128)(2,1)} %wv_hbm.1, ...), custom_call_target="tpu_custom_call" | custom-call | tf_op jit(solution)/shard_map/step/pallas_call | solution.py:427
  71.7 4.6 %write.1 = (bf16[128,49152]{1,0:T(8,128)(2,1)}, f32[1,128]{1,0:T(1,128)}, f32[1,128]{1,0:T(1,128)}, f32[1,128]{1,0:T(1,128)}) custom-call(bf16[128,49152]{1,0:T(8,128)(2,1)S(1)} %get-tuple-element.10.src, f32[8,128]{1,0:T(8,128)S(1)} %get-tuple-element.11.small), custom_call_target="tpu_custom_call" | custom-call | tf_op jit(solution)/shard_map/write/pallas_call | solution.py:448

commit v6 on v5

--- a/solution.py
+++ b/solution.py
@@ -12,16 +12,17 @@
 NC = 8
 CW = VL // NC
 GRID = 3072 // CW
-EARLY = 3
+EARLY = 4
 OWN = 7
 GROUP = 2
-SPLIT = 6
+NP = NC // 2
 CUTS = (0, 4, 7, 8)
 NS = len(CUTS) - 1
 NF = 4
 FW = FL // NF
 NJ = 4
 JW = D // NJ
+RS_ENDS = (1, 2, 3)
 HALF, PIECE = 64, 16
 NW = 4
 WW = VL // NW
@@ -39,7 +40,7 @@
           out, small,
           w, wv, hid, act, yf, yall, ysend, yrecv, psend, precv0, precv, xbuf, kept, statm, stats, offs, invt, tgtm, gain, temp, tgt,
           in_sem, wf_sem, wd_sem, wv_sem,
-          d2d_s, d2d_r, rs_s, rs_r, x_s, xa_r, xf_r, st_s, st_r, bulk_s, rxy, rd, pr, prd):
+          d2d_s, d2d_r, rs_s, rs_r, x_s, xa_r, xf_r, st_s, st_r, bulk_s, rxy, rd, rdl, pr, prd, prdl):
     me = lax.axis_index("tp")
     core = me % 2
     nx, ny, nd, pt = me ^ 2, me ^ 4, me ^ 6, me ^ 1
@@ -69,7 +70,8 @@
     hid_copy = load(hid_hbm, hid, in_sem.at[0])
     load_wf(0)
     small_copies = [load(temp_hbm, temp, in_sem.at[1]), load(tgt_hbm, tgt, in_sem.at[2]), load(gain_hbm, gain, in_sem.at[3])]
-    load_wf(1)
+    for b in range(1, NF):
+        load_wf(b)
 
     barrier = pltpu.get_barrier_semaphore()
     for k in range(1, 8):
@@ -79,13 +81,10 @@
     wd_copies, wv_copies = [], []
     for b in range(NF):
         wait_wf(b)
-        if b < NF - 2:
-            load_wf(b + 2)
-        else:
-            for j in range((b - NF + 2) * NJ // 2, (b - NF + 3) * NJ // 2):
-                wd_copies.append(load_wd(j))
-            if b == NF - 1:
-                wv_copies.append(load_wv(0))
+        for j in range(b * NJ // NF, (b + 1) * NJ // NF):
+            wd_copies.append(load_wd(j))
+        if b == NF - 1:
+            wv_copies.append(load_wv(0))
         g = jnp.dot(hid[...], w[:, b * FW:(b + 1) * FW], preferred_element_type=F32)
         u = jnp.dot(hid[...], w[:, FL + b * FW:FL + (b + 1) * FW], preferred_element_type=F32)
         act[:, b * FW:(b + 1) * FW] = (jax.nn.silu(g) * u).astype(BF16)
@@ -131,15 +130,18 @@
 
     for j in range(1, NJ):
         cols = slice(j * JW, (j + 1) * JW)
-        got = pl.ds((j - 1) * JW, JW)
         d2d[j - 1].wait_recv()
         part = yf[pl.ds(keep, HALF), cols] + yrecv[:, (j - 1) * JW:j * JW].astype(F32)
         yf[pl.ds(keep, HALF), cols] = part
         psend[:, (j - 1) * JW:j * JW] = part.astype(BF16)
-        for s, dev in enumerate((nd, nx, ny)):
-            remote(psend.at[pl.ds(piece(dev), PIECE), got], precv.at[pl.ds(s * PIECE, PIECE), got], rs_s, rs_r, dev).start()
-
-    rs_all = remote(hid.at[pl.ds(0, HALF), :], hid.at[pl.ds(0, HALF), :], rs_s, rs_r, nx)
+        if j in RS_ENDS:
+            start = max([0] + [e for e in RS_ENDS if e < j])
+            got = pl.ds(start * JW, (j - start) * JW)
+            for s, dev in enumerate((nd, nx, ny)):
+                remote(psend.at[pl.ds(piece(dev), PIECE), got], precv.at[pl.ds(s * PIECE, PIECE), got], rs_s, rs_r, dev).start()
+
+    bytes_in = hid.at[pl.ds(0, (7 * JW + 3 * (D - JW)) * PIECE // D), :]
+    rs_all = remote(bytes_in, bytes_in, rs_s, rs_r, nx)
     rs_all.wait_recv()
     mine = rows_of(me)
     y0 = yf[pl.ds(mine, PIECE), 0:JW]
@@ -165,16 +167,16 @@
         col = pl.multiple_of((i % GRID) * CW, CW)
         return row, pl.ds(col, CW)
 
-    def chunk(dev, i):
-        row, cols = place(dev, i)
-        return w.at[pl.ds(row, 128), cols]
-
-    def own_start(i, first, count):
-        row, cols = place(me, i)
-        ref = w.at[pl.ds(row + first, count), cols]
-        remote(ref, ref, bulk_s, rxy.at[i], nx).start()
-        remote(ref, ref, bulk_s, rxy.at[i], ny).start()
-        remote(ref, ref, bulk_s, pr.at[i], pt).start()
+    def block(dev, i, first, count, chunks=1):
+        row, _ = place(dev, i)
+        col = pl.multiple_of((i % GRID) * CW, CW)
+        return w.at[pl.ds(row + first, count), pl.ds(col, chunks * CW)]
+
+    def own_start(i, first, count, chunks=1):
+        ref = block(me, i, first, count, chunks)
+        remote(ref, ref, bulk_s, rxy.at[i // 2], nx).start()
+        remote(ref, ref, bulk_s, rxy.at[i // 2], ny).start()
+        remote(ref, ref, bulk_s, pr.at[i // 2], pt).start()
 
     def logits(i, first, count):
         acc = jnp.dot(xbuf[first:first + count, :], wv[:, pl.ds(pl.multiple_of(i * CW, CW), CW)], preferred_element_type=F32)
@@ -240,13 +242,11 @@
         while ready * WW < (group[-1] + 1) * CW:
             wv_copies[ready].wait()
             ready += 1
-        block = [logits(i, 0, PIECE) for i in group]
-        for i, parts in zip(group, block):
+        for i, parts in [(i, logits(i, 0, PIECE)) for i in group]:
             put(i, 0, PIECE, parts, row_max(parts))
             for q, p in enumerate(parts):
                 kept[:, i * CW + q * 128:i * CW + (q + 1) * 128] = p
-        for i in group:
-            own_start(i, 0, PIECE)
+        own_start(start, 0, PIECE, len(group))
     for s, k in ((1, 2), (2, 4), (0, 6)):
         remote(xrow(k), xrow(k), x_s, xa_r.at[s], me ^ k).wait_recv()
         remote(xrow(k), xrow(k + 1), x_s, xf_r, pt).start()
@@ -276,16 +276,12 @@
     for k in range(1, 8):
         remote(stats.at[pl.ds(0, 16), :], stats.at[pl.ds(16 * k, 16), :], st_s, st_r, me ^ k).start()
 
-    def send_rest(i, _):
-        own_start(i, PIECE, B - PIECE)
-        return 0
-
-    def send_all(i, _):
-        own_start(i, 0, B)
-        return 0
-
-    lax.fori_loop(EARLY, OWN, send_rest, 0)
-    lax.fori_loop(OWN, NC, send_all, 0)
+    for i in range(EARLY, NC, 2):
+        if i + 1 < OWN:
+            own_start(i, PIECE, B - PIECE, 2)
+        else:
+            for n in (i, i + 1):
+                own_start(n, PIECE if n < OWN else 0, B - PIECE if n < OWN else B)
 
     others = stats.at[pl.ds(16, 112), :]
     st_all = remote(others, others, st_s, st_r, nx)
@@ -318,83 +314,66 @@
             val = w[pl.ds(row + k * PIECE, PIECE), cols].astype(F32) + off
             out[rows, pl.ds(pl.multiple_of(dev * VL + i * CW, CW), CW)] = val.astype(BF16)
 
-    def land(n):
-        return w.at[pl.ds(0, n * 128), pl.ds(0, CW)]
-
     def arrived(n, sem):
-        remote(land(n), land(n), bulk_s, sem, nx).wait_recv()
-
-    def forward(rel, i, sem, to):
-        ref = chunk(me ^ rel, i)
+        ref = w.at[pl.ds(0, n * PIECE), pl.ds(0, CW)]
+        remote(ref, ref, bulk_s, sem, nx).wait_recv()
+
+    def send(ref, sem, to):
         remote(ref, ref, bulk_s, sem, to).start()
 
-    def pieces(rel, i, n):
-        row, cols = place(me ^ rel, i)
-        return w.at[pl.ds(row + CUTS[n] * PIECE, (CUTS[n + 1] - CUTS[n]) * PIECE), cols]
-
-    def piece_sem(sems, i, n):
-        return sems.at[i if n == 0 else NC + (i - SPLIT) * (NS - 1) + n - 1]
-
-    def relay(rel, i, to):
-        if isinstance(i, int):
+    def both(rel, p):
+        fix(rel, 2 * p)
+        fix(rel, 2 * p + 1)
+
+    def arrivals(p, _):
+        arrived(32, rxy.at[p])
+        if isinstance(p, int):
             for n in range(NS):
-                ref = pieces(rel, i, n)
-                remote(ref, ref, bulk_s, piece_sem(rd, i, n), to).start()
-            remote(ref, ref, bulk_s, piece_sem(prd, i, NS - 1), to ^ 1).start()
+                first, count = CUTS[n] * PIECE, (CUTS[n + 1] - CUTS[n]) * PIECE
+                for rel, i, to in ((2, 2 * p, ny), (4, 2 * p + 1, nx)):
+                    ref = block(me ^ rel, i, first, count)
+                    send(ref, rdl.at[n], to)
+                    if n == NS - 1:
+                        send(ref, prdl.at[n], to ^ 1)
         else:
-            forward(rel, i, rd.at[i], to)
-
-    def arrivals(i, _):
-        arrived(2, rxy.at[i])
-        if isinstance(i, int):
-            relay(2, i, ny) if i % 2 == 0 else relay(4, i, nx)
-        else:
-            @pl.when(i % 2 == 0)
-            def _():
-                relay(2, i, ny)
-
-            @pl.when(i % 2 == 1)
-            def _():
-                relay(4, i, nx)
-
-        forward(2, i, pr.at[i], pt)
-        forward(4, i, pr.at[i], pt)
-        fix(0, i)
-        fix(2, i)
-        fix(4, i)
-        arrived(3, pr.at[i])
-        fix(1, i)
-        fix(3, i)
-        fix(5, i)
+            send(block(nx, 2 * p, 0, B), rd.at[p], ny)
+            send(block(ny, 2 * p + 1, 0, B), rd.at[p], nx)
+        send(block(nx, 2 * p, 0, B, 2), pr.at[p], pt)
+        send(block(ny, 2 * p, 0, B, 2), pr.at[p], pt)
+        both(0, p)
+        both(2, p)
+        both(4, p)
+        arrived(48, pr.at[p])
+        both(1, p)
+        both(3, p)
+        both(5, p)
         return 0
 
-    lax.fori_loop(0, SPLIT, arrivals, 0)
-    for i in range(SPLIT, NC):
-        arrivals(i, 0)
-
-    def diagonal(i, _):
-        arrived(1, rd.at[i])
-        forward(6, i, prd.at[i], pt)
-        fix(6, i)
-        arrived(1, prd.at[i])
-        fix(7, i)
-        return 0
-
-    lax.fori_loop(0, SPLIT, diagonal, 0)
-    def part(n):
-        return w.at[pl.ds(0, (CUTS[n + 1] - CUTS[n]) * PIECE), pl.ds(0, CW)]
-
+    lax.fori_loop(0, NP - 1, arrivals, 0)
+    arrivals(NP - 1, 0)
+
+    for p in range(NP - 1):
+        arrived(16, rd.at[p])
+        send(block(nd, 2 * p, 0, B, 2), prd.at[p], pt)
+        both(6, p)
+        if p:
+            arrived(16, prd.at[p - 1])
+            both(7, p - 1)
     for n in range(NS):
-        for i in range(SPLIT, NC):
-            remote(part(n), part(n), bulk_s, piece_sem(rd, i, n), nx).wait_recv()
-            if n < NS - 1:
-                ref = pieces(6, i, n)
-                remote(ref, ref, bulk_s, piece_sem(prd, i, n), pt).start()
-            fix(6, i, CUTS[n], CUTS[n + 1] - CUTS[n])
+        count = CUTS[n + 1] - CUTS[n]
+        arrived(2 * count, rdl.at[n])
+        if n < NS - 1:
+            send(block(nd, NC - 2, CUTS[n] * PIECE, count * PIECE, 2), prdl.at[n], pt)
+        for i in (NC - 2, NC - 1):
+            fix(6, i, CUTS[n], count)
+        if n == 0:
+            arrived(16, prd.at[NP - 2])
+            both(7, NP - 2)
     for n in range(NS):
-        for i in range(SPLIT, NC):
-            remote(part(n), part(n), bulk_s, piece_sem(prd, i, n), pt).wait_recv()
-            fix(7, i, CUTS[n], CUTS[n + 1] - CUTS[n])
+        count = CUTS[n + 1] - CUTS[n]
+        arrived(2 * count, prdl.at[n])
+        for i in (NC - 2, NC - 1):
+            fix(7, i, CUTS[n], count)
 
     def left(ref, sem):
         remote(ref, ref, sem, rs_r, nx).wait_send()
@@ -439,7 +418,7 @@
                 pltpu.VMEM((1, D), F32), pltpu.VMEM((1, B), F32), pltpu.VMEM((1, B), jnp.int32),
                 dma((4,)), dma((NF,)), dma((NJ,)), dma((NW,)),
                 dma, dma((NJ - 1,)), dma, dma, dma, dma((3,)), dma, dma, dma, dma,
-                dma((NC,)), dma((NC + (NC - SPLIT) * (NS - 1),)), dma((NC,)), dma((NC + (NC - SPLIT) * (NS - 1),)),
+                dma((NP,)), dma((NP - 1,)), dma((NS,)), dma((NP,)), dma((NP - 1,)), dma((NS,)),
             ],
             compiler_params=pltpu.CompilerParams(collective_id=0, has_side_effects=True, vmem_limit_bytes=49 << 20),
             name="step",

time: 76.4 us -> 75.7 us (level)
  no operation moved by 1% of the time
where the time goes in v6:
time: 75.7 us; the launch traced here: 75.6 us
  Pallas kernels  75 us (99%)
    pallas_call x1, Pallas kernels, device_step(): pl.pallas_call(_main, out_shape=(pltpu.VMEM((B, V), BF16), pltpu.VMEM((8,...  70.4 us
    pallas_call x1, Pallas kernels, device_step(): pl.pallas_call(_write, out_shape=(jax.ShapeDtypeStruct((B, V), BF16), row...  4.6 us

profile of v6, /device:TPU:0, one launch (start us, length us, event | category | flops | bytes accessed | tf_op | source)
XLA Modules:
  0.0 75.6 jit_solution(7904503587658800608)
XLA Ops:
  0.6 70.4 %step.1 = (bf16[128,49152]{1,0:T(8,128)(2,1)S(1)}, f32[8,128]{1,0:T(8,128)S(1)}) custom-call(bf16[128,2048]{1,0:T(8,128)(2,1)} %hid_hbm.1, bf16[2048,1024]{1,0:T(8,128)(2,1)} %wg_hbm.1, bf16[2048,1024]{1,0:T(8,128)(2,1)} %wu_hbm.1, bf16[1024,2048]{1,0:T(8,128)(2,1)} %wd_hbm.1, f32[1,2048]{1,0:T(1,128)} %bitcast.6, bf16[2048,6144]{1,0:T(8,128)(2,1)} %wv_hbm.1, ...), custom_call_target="tpu_custom_call" | custom-call | tf_op jit(solution)/shard_map/step/pallas_call | solution.py:406
  71.0 4.6 %write.1 = (bf16[128,49152]{1,0:T(8,128)(2,1)}, f32[1,128]{1,0:T(1,128)}, f32[1,128]{1,0:T(1,128)}, f32[1,128]{1,0:T(1,128)}) custom-call(bf16[128,49152]{1,0:T(8,128)(2,1)S(1)} %get-tuple-element.10.src, f32[8,128]{1,0:T(8,128)S(1)} %get-tuple-element.11.small), custom_call_target="tpu_custom_call" | custom-call | tf_op jit(solution)/shard_map/write/pallas_call | solution.py:427

commit v7 on v6

--- a/solution.py
+++ b/solution.py
@@ -16,10 +16,11 @@
 OWN = 7
 GROUP = 2
 NP = NC // 2
-CUTS = (0, 4, 7, 8)
+CUTS = (0, 5, 7, 8)
 NS = len(CUTS) - 1
-NF = 4
-FW = FL // NF
+FCUTS = (0, 256, 768, 1024)
+NF = len(FCUTS) - 1
+WD_AT = (1, 2, 4)
 NJ = 4
 JW = D // NJ
 RS_ENDS = (1, 2, 3)
@@ -55,11 +56,12 @@
 
     def load_wf(b):
         for t, ref in enumerate((wg_hbm, wu_hbm)):
-            load(ref.at[:, pl.ds(b * FW, FW)], w.at[:, pl.ds(t * FL + b * FW, FW)], wf_sem.at[b])
+            start, width = FCUTS[b], FCUTS[b + 1] - FCUTS[b]
+            load(ref.at[:, pl.ds(start, width)], w.at[:, pl.ds(t * FL + start, width)], wf_sem.at[b])
 
     def wait_wf(b):
-        both = w.at[:, pl.ds(0, 2 * FW)]
-        pltpu.make_async_copy(wv_hbm.at[:, pl.ds(0, 2 * FW)], both, wf_sem.at[b]).wait()
+        width = 2 * (FCUTS[b + 1] - FCUTS[b])
+        pltpu.make_async_copy(wv_hbm.at[:, pl.ds(0, width)], w.at[:, pl.ds(0, width)], wf_sem.at[b]).wait()
 
     def load_wd(j):
         return load(wd_hbm.at[:, pl.ds(j * JW, JW)], w.at[pl.ds(j % 2 * FL, FL), pl.ds(2 * FL + j // 2 * JW, JW)], wd_sem.at[j])
@@ -81,13 +83,11 @@
     wd_copies, wv_copies = [], []
     for b in range(NF):
         wait_wf(b)
-        for j in range(b * NJ // NF, (b + 1) * NJ // NF):
+        for j in range(len(wd_copies), WD_AT[b]):
             wd_copies.append(load_wd(j))
-        if b == NF - 1:
-            wv_copies.append(load_wv(0))
-        g = jnp.dot(hid[...], w[:, b * FW:(b + 1) * FW], preferred_element_type=F32)
-        u = jnp.dot(hid[...], w[:, FL + b * FW:FL + (b + 1) * FW], preferred_element_type=F32)
-        act[:, b * FW:(b + 1) * FW] = (jax.nn.silu(g) * u).astype(BF16)
+        g = jnp.dot(hid[...], w[:, FCUTS[b]:FCUTS[b + 1]], preferred_element_type=F32)
+        u = jnp.dot(hid[...], w[:, FL + FCUTS[b]:FL + FCUTS[b + 1]], preferred_element_type=F32)
+        act[:, FCUTS[b]:FCUTS[b + 1]] = (jax.nn.silu(g) * u).astype(BF16)
 
     def rows_of(dev):
         return pl.multiple_of((dev % 2) * HALF + (dev // 2) * PIECE, PIECE)
@@ -97,8 +97,8 @@
     d2d = []
     for j in range(NJ):
         wd_copies[j].wait()
-        if j < NW - 1:
-            wv_copies.append(load_wv(j + 1))
+        if j < NW:
+            wv_copies.append(load_wv(j))
         wd = w[j % 2 * FL:(j % 2 + 1) * FL, 2 * FL + j // 2 * JW:2 * FL + (j // 2 + 1) * JW]
         yf[:, j * JW:(j + 1) * JW] = jnp.dot(act[...], wd, preferred_element_type=F32)
         if j == 0:
@@ -114,7 +114,7 @@
         c.start()
         d2d.append(c)
 
-    for n in range(min(NJ + 1, NW), NW):
+    for n in range(min(NJ, NW), NW):
         wv_copies.append(load_wv(n))
     for c in small_copies:
         c.wait()
@@ -389,7 +389,9 @@
     step = B // 16
     cs = [pltpu.make_async_copy(small.at[pl.ds(k, 1), :], o, sem.at[k]) for k, o in enumerate((o0, o1, o2))]
     for k in range(16):
-        pltpu.make_async_copy(src.at[pl.ds(k * step, step)], out.at[pl.ds(k * step, step)], sem.at[3]).start()
+        for c in range(4):
+            at = (pl.ds(k * step, step), pl.ds(c * (V // 4), V // 4))
+            pltpu.make_async_copy(src.at[at], out.at[at], sem.at[3]).start()
     for c in cs:
         c.start()
     for c in cs:

time: 75.7 us -> 75.4 us (level)
  no operation moved by 1% of the time
where the time goes in v7:
time: 75.4 us; the launch traced here: 75.3 us
  Pallas kernels  74.7 us (99%)
    pallas_call x1, Pallas kernels, device_step(): pl.pallas_call(_main, out_shape=(pltpu.VMEM((B, V), BF16), pltpu.VMEM((8,...  70.2 us
    pallas_call x1, Pallas kernels, device_step(): pl.pallas_call(_write, out_shape=(jax.ShapeDtypeStruct((B, V), BF16), row...  4.55 us

profile of v7, /device:TPU:0, one launch (start us, length us, event | category | flops | bytes accessed | tf_op | source)
XLA Modules:
  0.0 75.3 jit_solution(4030474717282621748)
XLA Ops:
  0.6 70.2 %step.1 = (bf16[128,49152]{1,0:T(8,128)(2,1)S(1)}, f32[8,128]{1,0:T(8,128)S(1)}) custom-call(bf16[128,2048]{1,0:T(8,128)(2,1)} %hid_hbm.1, bf16[2048,1024]{1,0:T(8,128)(2,1)} %wg_hbm.1, bf16[2048,1024]{1,0:T(8,128)(2,1)} %wu_hbm.1, bf16[1024,2048]{1,0:T(8,128)(2,1)} %wd_hbm.1, f32[1,2048]{1,0:T(1,128)} %bitcast.6, bf16[2048,6144]{1,0:T(8,128)(2,1)} %wv_hbm.1, ...), custom_call_target="tpu_custom_call" | custom-call | tf_op jit(solution)/shard_map/step/pallas_call | solution.py:408
  70.8 4.5 %write.1 = (bf16[128,49152]{1,0:T(8,128)(2,1)}, f32[1,128]{1,0:T(1,128)}, f32[1,128]{1,0:T(1,128)}, f32[1,128]{1,0:T(1,128)}) custom-call(bf16[128,49152]{1,0:T(8,128)(2,1)S(1)} %get-tuple-element.10.src, f32[8,128]{1,0:T(8,128)S(1)} %get-tuple-element.11.small), custom_call_target="tpu_custom_call" | custom-call | tf_op jit(solution)/shard_map/write/pallas_call | solution.py:429

commit v8 on v7

--- a/solution.py
+++ b/solution.py
@@ -16,14 +16,13 @@
 OWN = 7
 GROUP = 2
 NP = NC // 2
-CUTS = (0, 5, 7, 8)
+CUTS = (0, 6, 7, 8)
 NS = len(CUTS) - 1
 FCUTS = (0, 256, 768, 1024)
 NF = len(FCUTS) - 1
 WD_AT = (1, 2, 4)
 NJ = 4
 JW = D // NJ
-RS_ENDS = (1, 2, 3)
 HALF, PIECE = 64, 16
 NW = 4
 WW = VL // NW
@@ -108,9 +107,9 @@
                 remote(yall.at[pl.ds(rows_of(me ^ k), PIECE), :], precv0.at[pl.ds((k - 1) * PIECE, PIECE), :],
                        rs_s, rs_r, me ^ k).start()
             continue
-        ysend[:, (j - 1) * JW:j * JW] = yf[pl.ds(give, HALF), j * JW:(j + 1) * JW].astype(BF16)
-        cols = pl.ds((j - 1) * JW, JW)
-        c = remote(ysend.at[:, cols], yrecv.at[:, cols], d2d_s, d2d_r.at[j - 1], pt)
+        rows = pl.ds((j - 1) * HALF, HALF)
+        ysend[rows, :] = yf[pl.ds(give, HALF), j * JW:(j + 1) * JW].astype(BF16)
+        c = remote(ysend.at[rows, :], yrecv.at[rows, :], d2d_s, d2d_r.at[j - 1], pt)
         c.start()
         d2d.append(c)
 
@@ -131,14 +130,12 @@
     for j in range(1, NJ):
         cols = slice(j * JW, (j + 1) * JW)
         d2d[j - 1].wait_recv()
-        part = yf[pl.ds(keep, HALF), cols] + yrecv[:, (j - 1) * JW:j * JW].astype(F32)
+        part = yf[pl.ds(keep, HALF), cols] + yrecv[(j - 1) * HALF:j * HALF, :].astype(F32)
         yf[pl.ds(keep, HALF), cols] = part
-        psend[:, (j - 1) * JW:j * JW] = part.astype(BF16)
-        if j in RS_ENDS:
-            start = max([0] + [e for e in RS_ENDS if e < j])
-            got = pl.ds(start * JW, (j - start) * JW)
-            for s, dev in enumerate((nd, nx, ny)):
-                remote(psend.at[pl.ds(piece(dev), PIECE), got], precv.at[pl.ds(s * PIECE, PIECE), got], rs_s, rs_r, dev).start()
+        psend[(j - 1) * HALF:j * HALF, :] = part.astype(BF16)
+        for s, dev in enumerate((nd, nx, ny)):
+            remote(psend.at[pl.ds((j - 1) * HALF + piece(dev), PIECE), :], precv.at[pl.ds(((j - 1) * 3 + s) * PIECE, PIECE), :],
+                   rs_s, rs_r, dev).start()
 
     bytes_in = hid.at[pl.ds(0, (7 * JW + 3 * (D - JW)) * PIECE // D), :]
     rs_all = remote(bytes_in, bytes_in, rs_s, rs_r, nx)
@@ -147,10 +144,14 @@
     y0 = yf[pl.ds(mine, PIECE), 0:JW]
     for k in range(7):
         y0 = y0 + precv0[k * PIECE:(k + 1) * PIECE, :].astype(F32)
-    y1 = yf[pl.ds(mine, PIECE), JW:D]
-    for s in range(3):
-        y1 = y1 + precv[s * PIECE:(s + 1) * PIECE, :].astype(F32)
-    y = jnp.concatenate([y0, y1], axis=-1)
+    ys = [y0]
+    for j in range(1, NJ):
+        yj = yf[pl.ds(mine, PIECE), j * JW:(j + 1) * JW]
+        for s in range(3):
+            row = ((j - 1) * 3 + s) * PIECE
+            yj = yj + precv[row:row + PIECE, :].astype(F32)
+        ys.append(yj)
+    y = jnp.concatenate(ys, axis=-1)
     res = hid[pl.ds(mine, PIECE), :].astype(F32) + y
     inv_rms = lax.rsqrt(jnp.mean(res * res, axis=-1, keepdims=True) + NORM_EPS)
     xbuf[0:PIECE, :] = (gain[...] * res * inv_rms).astype(BF16)
@@ -412,9 +413,9 @@
             out_specs=(vmem, vmem),
             scratch_shapes=[
                 pltpu.VMEM((2048, 3072), BF16), pltpu.VMEM((D, VL), BF16), pltpu.VMEM((B, D), BF16),
-                pltpu.VMEM((B, FL), BF16), pltpu.VMEM((B, D), F32), pltpu.VMEM((B, JW), BF16), pltpu.VMEM((HALF, D - JW), BF16),
-                pltpu.VMEM((HALF, D - JW), BF16), pltpu.VMEM((HALF, D - JW), BF16), pltpu.VMEM((7 * PIECE, JW), BF16),
-                pltpu.VMEM((3 * PIECE, D - JW), BF16),
+                pltpu.VMEM((B, FL), BF16), pltpu.VMEM((B, D), F32), pltpu.VMEM((B, JW), BF16), pltpu.VMEM(((NJ - 1) * HALF, JW), BF16),
+                pltpu.VMEM(((NJ - 1) * HALF, JW), BF16), pltpu.VMEM(((NJ - 1) * HALF, JW), BF16), pltpu.VMEM((7 * PIECE, JW), BF16),
+                pltpu.VMEM(((NJ - 1) * 3 * PIECE, JW), BF16),
                 pltpu.VMEM((B, D), BF16), pltpu.VMEM((PIECE, OWN * CW), F32), pltpu.VMEM((128, 128), F32), pltpu.VMEM((128, 128), F32),
                 pltpu.VMEM((128, 128), F32), pltpu.VMEM((128, 128), F32), pltpu.VMEM((128, 128), jnp.int32),
                 pltpu.VMEM((1, D), F32), pltpu.VMEM((1, B), F32), pltpu.VMEM((1, B), jnp.int32),

time: 75.4 us -> 75.4 us (level)
  no operation moved by 1% of the time
where the time goes in v8:
time: 75.4 us; the launch traced here: 75.3 us
  Pallas kernels  74.6 us (99%)
    pallas_call x1, Pallas kernels, device_step(): pl.pallas_call(_main, out_shape=(pltpu.VMEM((B, V), BF16), pltpu.VMEM((8,...  70.1 us
    pallas_call x1, Pallas kernels, device_step(): pl.pallas_call(_write, out_shape=(jax.ShapeDtypeStruct((B, V), BF16), row...  4.55 us

profile of v8, /device:TPU:0, one launch (start us, length us, event | category | flops | bytes accessed | tf_op | source)
XLA Modules:
  0.0 75.3 jit_solution(6426975339767009986)
XLA Ops:
  0.6 70.1 %step.1 = (bf16[128,49152]{1,0:T(8,128)(2,1)S(1)}, f32[8,128]{1,0:T(8,128)S(1)}) custom-call(bf16[128,2048]{1,0:T(8,128)(2,1)} %hid_hbm.1, bf16[2048,1024]{1,0:T(8,128)(2,1)} %wg_hbm.1, bf16[2048,1024]{1,0:T(8,128)(2,1)} %wu_hbm.1, bf16[1024,2048]{1,0:T(8,128)(2,1)} %wd_hbm.1, f32[1,2048]{1,0:T(1,128)} %bitcast.6, bf16[2048,6144]{1,0:T(8,128)(2,1)} %wv_hbm.1, ...), custom_call_target="tpu_custom_call" | custom-call | tf_op jit(solution)/shard_map/step/pallas_call | solution.py:409
  70.7 4.5 %write.1 = (bf16[128,49152]{1,0:T(8,128)(2,1)}, f32[1,128]{1,0:T(1,128)}, f32[1,128]{1,0:T(1,128)}, f32[1,128]{1,0:T(1,128)}) custom-call(bf16[128,49152]{1,0:T(8,128)(2,1)S(1)} %get-tuple-element.10.src, f32[8,128]{1,0:T(8,128)S(1)} %get-tuple-element.11.small), custom_call_target="tpu_custom_call" | custom-call | tf_op jit(solution)/shard_map/write/pallas_call | solution.py:430

commit v9 on v8

--- a/solution.py
+++ b/solution.py
@@ -24,7 +24,7 @@
 NJ = 4
 JW = D // NJ
 HALF, PIECE = 64, 16
-NW = 4
+NW = 2
 WW = VL // NW
 
 
@@ -390,8 +390,8 @@
     step = B // 16
     cs = [pltpu.make_async_copy(small.at[pl.ds(k, 1), :], o, sem.at[k]) for k, o in enumerate((o0, o1, o2))]
     for k in range(16):
-        for c in range(4):
-            at = (pl.ds(k * step, step), pl.ds(c * (V // 4), V // 4))
+        for c in range(8):
+            at = (pl.ds(k * step, step), pl.ds(c * (V // 8), V // 8))
             pltpu.make_async_copy(src.at[at], out.at[at], sem.at[3]).start()
     for c in cs:
         c.start()

time: 75.4 us -> 75.4 us (level)
  no operation moved by 1% of the time
where the time goes in v9:
time: 75.4 us; the launch traced here: 75.3 us
  Pallas kernels  74.6 us (99%)
    pallas_call x1, Pallas kernels, device_step(): pl.pallas_call(_main, out_shape=(pltpu.VMEM((B, V), BF16), pltpu.VMEM((8,...  70.1 us
    pallas_call x1, Pallas kernels, device_step(): pl.pallas_call(_write, out_shape=(jax.ShapeDtypeStruct((B, V), BF16), row...  4.54 us

profile of v9, /device:TPU:0, one launch (start us, length us, event | category | flops | bytes accessed | tf_op | source)
XLA Modules:
  0.0 75.3 jit_solution(18199624293515926532)
XLA Ops:
  0.6 70.1 %step.1 = (bf16[128,49152]{1,0:T(8,128)(2,1)S(1)}, f32[8,128]{1,0:T(8,128)S(1)}) custom-call(bf16[128,2048]{1,0:T(8,128)(2,1)} %hid_hbm.1, bf16[2048,1024]{1,0:T(8,128)(2,1)} %wg_hbm.1, bf16[2048,1024]{1,0:T(8,128)(2,1)} %wu_hbm.1, bf16[1024,2048]{1,0:T(8,128)(2,1)} %wd_hbm.1, f32[1,2048]{1,0:T(1,128)} %bitcast.6, bf16[2048,6144]{1,0:T(8,128)(2,1)} %wv_hbm.1, ...), custom_call_target="tpu_custom_call" | custom-call | tf_op jit(solution)/shard_map/step/pallas_call | solution.py:409
  70.7 4.5 %write.1 = (bf16[128,49152]{1,0:T(8,128)(2,1)}, f32[1,128]{1,0:T(1,128)}, f32[1,128]{1,0:T(1,128)}, f32[1,128]{1,0:T(1,128)}) custom-call(bf16[128,49152]{1,0:T(8,128)(2,1)S(1)} %get-tuple-element.10.src, f32[8,128]{1,0:T(8,128)S(1)} %get-tuple-element.11.small), custom_call_target="tpu_custom_call" | custom-call | tf_op jit(solution)/shard_map/write/pallas_call | solution.py:430
